TPU v7x, 16 devices: a whole 2x2x2 slice. The times are simulated.
16 devices in a mesh: dz: 2 (over z), dy: 2 (over y), dx: 4 (over x, core).
Axes of the slice: x: 2, y: 2, z: 2, core: 2. Of those that a mesh axis runs over, the one named last changes fastest.
Arguments:
- g_emb: float32 [16, 2048, 768], P(('dz', 'dy', 'dx'))
- g_attn: float32 [16, 1, 4, 768, 768], P(('dz', 'dy', 'dx'))
- g_in: float32 [16, 1, 768, 2048], P(('dz', 'dy', 'dx'))
- g_out: float32 [16, 1, 2048, 768], P(('dz', 'dy', 'dx'))
- g_vecd: float32 [16, 1, 9, 768], P(('dz', 'dy', 'dx'))
- g_vecf: float32 [16, 1, 2048], P(('dz', 'dy', 'dx'))
- opt_m: float32 [7088128], P(('dz', 'dy', 'dx'))
- opt_v: float32 [7088128], P(('dz', 'dy', 'dx'))
- master: float32 [7088128], P(('dz', 'dy', 'dx'))
- tok_ids: int32 [262144], P(('dz', 'dy', 'dx'))
- act_in: bfloat16 [262144, 768], P(('dz', 'dy', 'dx'))
Outputs:
- output 1: float32 [7088128], P(('dz', 'dy', 'dx'))
- output 2: float32 [7088128], P(('dz', 'dy', 'dx'))
- output 3: float32 [7088128], P(('dz', 'dy', 'dx'))
- output 4: bfloat16 [2048, 768], replicated
- output 5: bfloat16 [1, 4, 768, 768], replicated
- output 6: bfloat16 [1, 768, 2048], replicated
- output 7: bfloat16 [1, 2048, 768], replicated
- output 8: bfloat16 [1, 9, 768], replicated
- output 9: bfloat16 [1, 2048], replicated
- output 10: bfloat16 [262144, 768], P(('dz', 'dy', 'dx'))
All inputs are finite; a program needn't handle non-finite values.
Results may differ from a plain program's by a relative error of at most 0.001.
Values are sent between devices in bfloat16 or wider.
A program may use at most 1 GiB of HBM per device.

v0:
```python
import math
import jax
import jax.numpy as jnp
from jax import lax
from jax.sharding import PartitionSpec as P

LEARN_RATE = 0.002
BETA_ONE = 0.9
BETA_TWO = 0.95
ADAM_EPS = 1e-8
ADAM_STEP = 2
AXES = ("dz", "dy", "dx")
GRAD_RANKS = (3, 5, 4, 4, 4, 3)


def adam_update(grad_vals, opt_m, opt_v, master):
    m_new = BETA_ONE * opt_m + (1.0 - BETA_ONE) * grad_vals
    v_new = BETA_TWO * opt_v + (1.0 - BETA_TWO) * grad_vals * grad_vals
    m_hat = m_new / (1.0 - BETA_ONE ** ADAM_STEP)
    v_hat = v_new / (1.0 - BETA_TWO ** ADAM_STEP)
    w_new = master - LEARN_RATE * m_hat / (jnp.sqrt(v_hat) + ADAM_EPS)
    return m_new, v_new, w_new


def split_flat(flat_vals, shapes):
    pieces = []
    offset = 0
    for tensor_shape in shapes:
        elem_count = math.prod(tensor_shape)
        pieces.append(flat_vals[offset:offset + elem_count].reshape(tensor_shape))
        offset = offset + elem_count
    return pieces


def ffn_block(wb_emb, w_in, b_in, w_out, b_out, tok_ids, act_in):
    emb_rows = jnp.take(wb_emb, tok_ids, axis=0).astype(jnp.float32)
    hidden = (emb_rows * math.sqrt(wb_emb.shape[1]) + act_in.astype(jnp.float32)).astype(jnp.bfloat16)
    pre_act = jnp.dot(hidden, w_in, preferred_element_type=jnp.float32) + b_in.astype(jnp.float32)
    inner_act = jax.nn.gelu(pre_act, approximate=True).astype(jnp.bfloat16)
    return (jnp.dot(inner_act, w_out, preferred_element_type=jnp.float32) + b_out.astype(jnp.float32)).astype(jnp.bfloat16)


def solution(mesh):
    devices = math.prod([mesh.shape[axis_name] for axis_name in AXES])

    def device_step(g_emb, g_attn, g_in, g_out, g_vecd, g_vecf, opt_m, opt_v, master, tok_ids, act_in):
        grad_list = [g_emb, g_attn, g_in, g_out, g_vecd, g_vecf]
        shapes = [grad_arr.shape[1:] for grad_arr in grad_list]
        param_count = sum(math.prod(tensor_shape) for tensor_shape in shapes)
        shard_len = opt_m.shape[0]
        local_flat = jnp.concatenate([grad_arr.reshape(-1) for grad_arr in grad_list])
        local_flat = jnp.pad(local_flat, (0, shard_len * devices - param_count))
        grad_shard = lax.psum_scatter(local_flat, AXES, scatter_dimension=0, tiled=True) / devices
        m_new, v_new, w_new = adam_update(grad_shard, opt_m, opt_v, master)
        full_half = lax.all_gather(w_new.astype(jnp.bfloat16), AXES, axis=0, tiled=True)
        wb_emb, wb_attn, wb_in, wb_out, wb_vecd, wb_vecf = split_flat(full_half, shapes)
        y_out = ffn_block(wb_emb, wb_in[0], wb_vecf[0], wb_out[0], wb_vecd[0, 8], tok_ids, act_in)
        return (m_new, v_new, w_new, wb_emb, wb_attn, wb_in, wb_out, wb_vecd, wb_vecf, y_out)

    grad_specs = tuple(P(AXES, *([None] * (grad_rank - 1))) for grad_rank in GRAD_RANKS)
    in_specs = grad_specs + (P(AXES), P(AXES), P(AXES), P(AXES), P(AXES, None))
    out_specs = (P(AXES), P(AXES), P(AXES), P(), P(), P(), P(), P(), P(), P(AXES, None))
    return jax.shard_map(device_step, mesh=mesh, in_specs=in_specs, out_specs=out_specs, check_vma=False)
```

profile of v0, /device:TPU:0, one launch (start us, length us, event | category | flops | bytes accessed | tf_op | source)
XLA Modules:
  0.0 1075.6 jit_solution(12770257973791398423)
XLA Ops:
  7.2 0.0 all-reduce.4.cloned.1.call-start
  7.2 0.8 reduce
  8.1 6.9 reshape.77
  14.9 6.9 copy.21
  21.8 6.9 reshape.80
  28.7 10.7 reshape.78
  39.5 0.0 copy-start.1
  39.5 3.2 constant_dynamic-update-slice_fusion.5
  42.7 2.3 copy-done.1
  45.0 1.3 constant_dynamic-update-slice_fusion.4
  46.3 0.0 slice-start.1
  46.3 0.0 copy-start.6
  46.3 0.0 slice-start.2
  46.3 3.4 constant_dynamic-update-slice_fusion.3
  49.7 0.6 slice-done.1
  50.3 0.7 slice-done.2
  51.0 0.8 constant_dynamic-update-slice_fusion.2
  51.9 0.0 copy-done.6
  51.9 10.0 pad.4
  61.9 0.0 copy-start.3
  61.9 0.0 copy-start.4
  61.9 0.0 all-reduce.4.cloned.1.call-update
  61.9 0.2 all-gather.3.cloned.1.call-start
  62.1 277.4 %all-reduce.4.cloned.1.call-done = f32[7088128]{0:T(1024)} async-done(((f32[7088128]{0:T(1024)}), f32[7088128]{0:T(1024)}) %all-reduce.4.cloned.1.call-update) | async-done | bytes 28352528
  339.6 0.0 copy-done.3
  339.6 0.0 copy-done.4
  339.6 5.9 fusion.22
  345.5 10.8 %reshape.99 = bf16[1,1,443008]{2,1,0:T(2,128)(2,1)} reshape(bf16[443008]{0:T(1024)(128)(2,1)S(1)} %get-tuple-element.10) | data formatting | bytes 1772032
  356.4 0.0 all-gather.3.cloned.1.call-update
  356.4 0.9 compare_and_fusion
  357.2 0.9 fusion.12
  358.1 112.5 %all-gather.3.cloned.1.call-done = bf16[16,1,443008]{2,1,0:T(2,128)(2,1)} async-done(((bf16[1,1,443008]{2,1,0:T(2,128)(2,1)}), bf16[16,1,443008]{2,1,0:T(2,128)(2,1)}) %all-gather.3.cloned.1.call-update) | async-done | bytes 14176272 | tf_op jit(solution)/shard_map/all_gather | solution.py:55
  470.6 292.8 %reduce.1 = bf16[16,443008]{1,0:T(8,128)(2,1)} reduce(bf16[16,1,443008]{2,1,0:T(2,128)(2,1)} %all-gather.3.cloned.1.call-done, bf16[]{:T(256)} %constant.64), dimensions={1}, to_apply=%all-gather.reduce_sub_computation | reduce | bytes 28352514 | tf_op jit(solution)/shard_map/all_gather | solution.py:55
  763.4 33.3 %reshape.100 = bf16[7088128]{0:T(1024)(128)(2,1)} reshape(bf16[16,443008]{1,0:T(8,128)(2,1)} %reduce.1) | data formatting | bytes 28352512
  796.7 0.7 slice_convert_fusion.1
  797.4 5.4 slice.42
  802.8 5.9 fusion.23
  808.7 0.0 slice-start
  808.7 6.6 squeeze_reshape.4
  815.2 6.4 reshape.86
  821.6 3.3 slice.37
  824.9 3.3 reshape.85
  828.2 0.6 reshape.88
  828.8 0.0 slice-done
  828.8 0.0 copy-start.5
  828.8 0.6 fusion.13
  829.4 0.0 copy-done.5
  829.4 5.1 reshape.83
  834.5 0.0 copy-start
  834.6 9.6 reshape.84
  844.2 67.8 %gather_fusion = bf16[16384,768]{1,0:T(8,128)(2,1)} fusion(bf16[2048,768]{1,0:T(8,128)(2,1)S(1)} %reshape.83, s32[16384]{0:T(1024)S(1)} %fusion.12), kind=kCustom, calls=%fused_computation | custom fusion | bytes 50397184 | tf_op jit(solution)/shard_map/jit(_take)/gather | solution.py:36
  912.0 0.0 copy-done
  912.0 0.0 copy-start.2
  912.0 0.0 copy-start.7
  912.0 95.7 %fusion.7.clone.4 = bf16[16384,2048]{1,0:T(8,128)(2,1)} fusion(bf16[768,2048]{1,0:T(8,128)(2,1)} %slice.37, f32[2048]{0:T(1024)S(1)} %get-tuple-element.14, bf16[16384,768]{1,0:T(8,128)(2,1)} %param.21, bf16[16384,768]{1,0:T(8,128)(2,1)} %gather_fusion, pred[16384]{0:T(1024)(128)(4,1)S(1)} %compare_and_fusion), kind=kOutput, calls=%fused_computation.9.clone.clone.clone.1 | convolution fusion | flops 51950649344 | bytes 120610816 | tf_op jit(solution)/shard_map/dot_general | solution.py:38
  1007.7 0.0 copy-done.2
  1007.7 0.0 copy-done.7
  1007.7 60.8 %add_convert_fusion = bf16[16384,768]{1,0:T(8,128)(2,1)} fusion(bf16[2048,768]{1,0:T(8,128)(2,1)S(1)} %copy-done.2, f32[768]{0:T(1024)S(1)} %copy-done.7, bf16[16384,2048]{1,0:T(8,128)(2,1)} %fusion.7.clone.4), kind=kOutput, calls=%fused_computation.10 | convolution fusion | flops 51564773376 | bytes 95423488 | tf_op jit(solution)/shard_map/dot_general | solution.py:40
  (5 shorter events, 0.1 us)
Async XLA Ops:
  7.2 332.4 %all-reduce.4.cloned.1.call-start = ((), (), s32[]{:S(2)}) async-start(), calls=%async_computation.1 | async-start | bytes 56705024
  39.5 5.5 copy-start.1
  46.3 4.0 slice-start.1
  46.3 5.6 copy-start.6
  46.3 4.7 slice-start.2
  61.9 277.7 %copy-start.3 = (f32[443008]{0:T(1024)S(1)}, f32[443008]{0:T(1024)}, u32[]{:S(2)}) copy-start(f32[443008]{0:T(1024)} %param.19) | copy-start | bytes 5316100
  61.9 277.7 %copy-start.4 = (f32[443008]{0:T(1024)S(1)}, f32[443008]{0:T(1024)}, u32[]{:S(2)}) copy-start(f32[443008]{0:T(1024)} %param.18) | copy-start | bytes 5316100
  61.9 408.7 %all-gather.3.cloned.1.call-start = ((), (), s32[]{:S(2)}) async-start(), calls=%async_computation | async-start | bytes 30124544 | tf_op jit(solution)/shard_map/all_gather | solution.py:55
  808.7 20.1 %slice-start = ((bf16[7088128]{0:T(1024)(128)(2,1)}), bf16[6912]{0:T(1024)(128)(2,1)S(1)}, s32[]{:S(2)}) async-start(bf16[7088128]{0:T(1024)(128)(2,1)} %reshape.100), calls=%async_computation.2 | async-start | bytes 28672 | tf_op jit(solution)/shard_map/slice | solution.py:30
  828.8 0.6 copy-start.5
  834.5 77.5 %copy-start = (bf16[2048,768]{1,0:T(8,128)(2,1)}, bf16[2048,768]{1,0:T(8,128)(2,1)S(1)}, u32[]{:S(2)}) copy-start(bf16[2048,768]{1,0:T(8,128)(2,1)S(1)} %reshape.83) | copy-start | bytes 9437188
  912.0 95.7 %copy-start.2 = (bf16[2048,768]{1,0:T(8,128)(2,1)S(1)}, bf16[2048,768]{1,0:T(8,128)(2,1)}, u32[]{:S(2)}) copy-start(bf16[2048,768]{1,0:T(8,128)(2,1)} %squeeze_reshape.4) | copy-start | bytes 9437188
  912.0 95.7 %copy-start.7 = (f32[768]{0:T(1024)S(1)}, f32[768]{0:T(1024)}, u32[]{:S(2)}) copy-start(f32[768]{0:T(1024)} %fusion.13) | copy-start | bytes 9220
Sparse Core Ops, SparseCore 0:
  62.0 277.4 all-reduce.3
  356.5 114.0 all-gather.2
where the time goes:
time: 1080 us
  waiting for transfers between devices  390 us (36%)
  other arithmetic  303 us (28%)
  local copies, waits for them, and re-layouts  212 us (20%)
  matrix products  157 us (15%)
  between operations  14.4 us (1%)
    all_gather x1, other arithmetic, device_step(): lax.all_gather(w_new.astype(jnp.bfloat16), AXES, axis=0, tiled=True)  293 us
    unnamed x3, waiting for transfers between devices  277 us
    all_gather x1, waiting for transfers between devices, device_step(): lax.all_gather(w_new.astype(jnp.bfloat16), AXES, axis=0, tiled=True)  112 us
    dot_general x1, matrix products, ffn_block(): jnp.dot(hidden, w_in, preferred_element_type=jnp.float32)  95.7 us
    gather x1, local copies, waits for them, and re-layouts, ffn_block(): emb_rows = jnp.take(wb_emb, tok_ids, axis=0).astype(jnp.float32)  67.8 us
    unnamed x28, local copies, waits for them, and re-layouts  63.3 us
    dot_general x1, matrix products, ffn_block(): jnp.dot(inner_act, w_out, preferred_element_type=jnp.float32)  60.8 us
    reshape x6, local copies, waits for them, and re-layouts, split_flat(): pieces.append(flat_vals[offset:offset + elem_count].reshape(tensor_shape))  25 us
  transfers between devices with their start and end apart: 2, of which 2 were waited for; matrix products, arithmetic and copies ran while one was open for 0% of the time, Pallas kernels for 0%

commit v1 on v0

v1 whole, which is shorter than its diff:
```python
import functools
import math

import jax
import jax.numpy as jnp
from jax import lax
from jax.experimental import pallas as pl
from jax.experimental.pallas import tpu as pltpu
from jax.sharding import PartitionSpec as P

LEARN_RATE = 0.002
BETA_ONE = 0.9
BETA_TWO = 0.95
ADAM_EPS = 1e-8
ADAM_STEP = 2
AXES = ("dz", "dy", "dx")
GRAD_RANKS = (3, 5, 4, 4, 4, 3)
MESH = pl.DeviceIdType.MESH

D = 768
FF = 2048
VOCAB = 2048
DEVICES = 16
LANES = 128
SHARD = 3461
PAD = 3472
PART_START = (0, 1152, 2304)
PART_ROWS = (1152, 1152, 1168)
PART_MAX = 1168
VMEM_MAX = 67_000_000

TENSORS = (
    (VOCAB, D, 0),
    (4 * D, D, VOCAB * D // LANES),
    (D, FF, (VOCAB * D + 4 * D * D) // LANES),
    (FF, D, (VOCAB * D + 4 * D * D + D * FF) // LANES),
)
VEC_BASE = (VOCAB * D + 4 * D * D + 2 * D * FF) // LANES
VEC_ROWS = DEVICES * SHARD - VEC_BASE


def flat_chunks():
    chunks = []
    for index, (rows, cols, base) in enumerate(TENSORS):
        step = 256 if cols == D else 128
        for start in range(0, rows, step):
            chunks.append((index, start, step))
    return chunks


def flatten_kernel(g_emb, g_attn, g_in, g_out, vec, flat_out, s_emb, s_attn, s_in, s_out, s_vec, flat, in_sem, out_sem):
    sources = (g_emb, g_attn, g_in, g_out)
    stages = (s_emb, s_attn, s_in, s_out)
    chunks = flat_chunks()

    def load(k):
        index, start, step = chunks[k]
        return pltpu.make_async_copy(
            sources[index].at[pl.ds(start, step)], stages[index].at[pl.ds(start, step)], in_sem.at[k])

    vec_load = pltpu.make_async_copy(vec, s_vec, in_sem.at[len(chunks)])
    for k in range(len(chunks)):
        load(k).start()
    vec_load.start()

    def put(owner):
        return pltpu.make_async_copy(flat.at[pl.ds(owner * PAD, PAD)], flat_out.at[owner], out_sem.at[owner])

    sent = 0
    for k, (index, start, step) in enumerate(chunks):
        _, cols, base = TENSORS[index]
        groups = cols // LANES
        stage = stages[index]
        load(k).wait()
        tile = start // 8
        last = (start + step) // 8
        while tile < last:
            first_row = base + tile * 8 * groups
            owner = first_row // SHARD
            fit = (SHARD * (owner + 1) - first_row) // (8 * groups)
            run = min(fit, last - tile)
            if run > 0:
                shift = base + (PAD - SHARD) * owner

                def body(t, carry, shift=shift, groups=groups, stage=stage):
                    row = pl.multiple_of(t * 8, 8)
                    for j in range(groups):
                        flat[pl.ds(shift + row * groups + j, 8, stride=groups), :] = (
                            stage[pl.ds(row, 8), j * LANES:(j + 1) * LANES])
                    return carry

                lax.fori_loop(tile, tile + run, body, 0, unroll=2)
                tile = tile + run
            else:
                for i in range(8):
                    for j in range(groups):
                        q = first_row + i * groups + j
                        p = q + (PAD - SHARD) * (q // SHARD)
                        flat[p:p + 1, :] = stage[tile * 8 + i:tile * 8 + i + 1, j * LANES:(j + 1) * LANES]
                tile = tile + 1
        done = (base + last * 8 * groups) // SHARD
        while sent < min(done, DEVICES - 1):
            put(sent).start()
            sent = sent + 1
    vec_load.wait()
    last_row = VEC_BASE + (PAD - SHARD) * (DEVICES - 1)
    flat[last_row:last_row + VEC_ROWS, :] = s_vec[...]
    while sent < DEVICES:
        put(sent).start()
        sent = sent + 1
    for owner in range(DEVICES):
        put(owner).wait()


def flatten(g_emb, g_attn, g_in, g_out, vec):
    chunk_count = len(flat_chunks())
    scratch = [pltpu.VMEM((rows, cols), jnp.float32) for rows, cols, _ in TENSORS]
    scratch += [
        pltpu.VMEM((VEC_ROWS, LANES), jnp.float32),
        pltpu.VMEM((DEVICES * PAD, LANES), jnp.float32),
        pltpu.SemaphoreType.DMA((chunk_count + 1,)),
        pltpu.SemaphoreType.DMA((DEVICES,)),
    ]
    return pl.pallas_call(
        flatten_kernel,
        out_shape=jax.ShapeDtypeStruct((DEVICES, PAD, LANES), jnp.float32),
        in_specs=[pl.BlockSpec(memory_space=pl.ANY)] * 5,
        out_specs=pl.BlockSpec(memory_space=pl.ANY),
        scratch_shapes=scratch,
        compiler_params=pltpu.CompilerParams(vmem_limit_bytes=VMEM_MAX),
        name="flatten",
    )(g_emb, g_attn, g_in, g_out, vec)


ORDERS = (("x", "y", "z"), ("y", "z", "x"), ("z", "x", "y"))
WEIGHT = {"z": 4, "y": 2, "x": 1}
HALF_ORDER = ((1, 1), (1, 0), (0, 1), (0, 0))
GATHER_ORDER = ((1, 0, 0), (0, 1, 0), (0, 0, 1), (1, 1, 0), (1, 0, 1), (0, 1, 1), (1, 1, 1))


def exchange_kernel(grad, opt_m, opt_v, master, m_new, v_new, w_new, gathered,
                    acc, pair, half, quarter, eighth, m_buf, v_buf, w_buf, wb,
                    load_sem, pair_send, pair_recv, half_send, half_recv, quarter_send, quarter_recv,
                    eighth_send, eighth_recv, state_sem, store_sem,
                    ring_send, ring_recv, share_send, share_recv, keep_sem):
    z, y, dx = lax.axis_index("dz"), lax.axis_index("dy"), lax.axis_index("dx")
    x, c = dx // 2, dx % 2
    mine = {"z": z, "y": y, "x": x}
    peers = {
        "c": {"dz": z, "dy": y, "dx": 2 * x + (1 - c)},
        "x": {"dz": z, "dy": y, "dx": 2 * (1 - x) + c},
        "y": {"dz": z, "dy": 1 - y, "dx": dx},
        "z": {"dz": 1 - z, "dy": y, "dx": dx},
    }

    def chip(part, bits):
        index = 0
        for axis, bit in zip(ORDERS[part], bits):
            index = index + WEIGHT[axis] * ((1 - mine[axis]) if bit else mine[axis])
        return index

    def rows(part):
        return pl.ds(PART_START[part], PART_ROWS[part])

    barrier = pltpu.get_barrier_semaphore()
    for peer in peers.values():
        pl.semaphore_signal(barrier, inc=1, device_id=peer, device_id_type=MESH)
    pl.semaphore_wait(barrier, 4)

    state = [
        pltpu.make_async_copy(opt_m, m_buf, state_sem.at[0]),
        pltpu.make_async_copy(opt_v, v_buf, state_sem.at[1]),
        pltpu.make_async_copy(master, w_buf, state_sem.at[2]),
    ]

    units = [(b1,) + rest for b1 in (1, 0) for rest in HALF_ORDER]
    parts = (0, 1, 2)

    def load(n, part):
        where = chip(part, units[n])
        return pltpu.make_async_copy(
            grad.at[where, c, rows(part)], acc.at[where, rows(part)], load_sem.at[n, part])

    def pair_copy(n, part):
        where = chip(part, units[n])
        return pltpu.make_async_remote_copy(
            src_ref=grad.at[where, 1 - c, rows(part)], dst_ref=pair.at[where, rows(part)],
            send_sem=pair_send.at[n, part], recv_sem=pair_recv.at[n, part],
            device_id=peers["c"], device_id_type=MESH)

    def half_copy(k, part):
        return pltpu.make_async_remote_copy(
            src_ref=acc.at[chip(part, (1,) + HALF_ORDER[k]), rows(part)],
            dst_ref=half.at[part, k, pl.ds(0, PART_ROWS[part])],
            send_sem=half_send.at[k, part], recv_sem=half_recv.at[k, part],
            device_id=peers[ORDERS[part][0]], device_id_type=MESH)

    def quarter_copy(k, part):
        return pltpu.make_async_remote_copy(
            src_ref=acc.at[chip(part, (0, 1, 1 - k)), rows(part)],
            dst_ref=quarter.at[part, k, pl.ds(0, PART_ROWS[part])],
            send_sem=quarter_send.at[k, part], recv_sem=quarter_recv.at[k, part],
            device_id=peers[ORDERS[part][1]], device_id_type=MESH)

    def eighth_copy(part):
        return pltpu.make_async_remote_copy(
            src_ref=acc.at[chip(part, (0, 0, 1)), rows(part)],
            dst_ref=eighth.at[part, pl.ds(0, PART_ROWS[part])],
            send_sem=eighth_send.at[part], recv_sem=eighth_recv.at[part],
            device_id=peers[ORDERS[part][2]], device_id_type=MESH)

    for n in range(8):
        for part in parts:
            load(n, part).start()
            pair_copy(n, part).start()
    for copy in state:
        copy.start()

    for n in range(8):
        for part in parts:
            load(n, part).wait()
            pair_copy(n, part).wait_recv()
            where = chip(part, units[n])
            acc[where, rows(part)] += pair[where, rows(part)]
            if n < 4:
                half_copy(n, part).start()
    for k in range(4):
        for part in parts:
            half_copy(k, part).wait_recv()
            where = chip(part, (0,) + HALF_ORDER[k])
            acc[where, rows(part)] += half[part, k, pl.ds(0, PART_ROWS[part])]
            if k < 2:
                quarter_copy(k, part).start()
    for k in range(2):
        for part in parts:
            quarter_copy(k, part).wait_recv()
            where = chip(part, (0, 0, 1 - k))
            acc[where, rows(part)] += quarter[part, k, pl.ds(0, PART_ROWS[part])]
            if k == 0:
                eighth_copy(part).start()

    for copy in state:
        copy.wait()

    here = 4 * z + 2 * y + x

    def ring_copy(bits, hop, part):
        flipped = tuple(1 - bit if n == hop else bit for n, bit in enumerate(bits))
        slot = flipped[0] * 4 + flipped[1] * 2 + flipped[2]
        where = chip(part, bits)
        return pltpu.make_async_remote_copy(
            src_ref=wb.at[where, rows(part)], dst_ref=wb.at[where, rows(part)],
            send_sem=ring_send.at[slot, part], recv_sem=ring_recv.at[slot, part],
            device_id=peers[ORDERS[part][hop]], device_id_type=MESH)

    def share_copy(bits, part):
        slot = bits[0] * 4 + bits[1] * 2 + bits[2]
        where = chip(part, bits)
        return pltpu.make_async_remote_copy(
            src_ref=wb.at[where, rows(part)], dst_ref=gathered.at[where, c, rows(part)],
            send_sem=share_send.at[slot, part], recv_sem=share_recv.at[slot, part],
            device_id=peers["c"], device_id_type=MESH)

    def keep_copy(bits, part):
        slot = bits[0] * 4 + bits[1] * 2 + bits[2]
        where = chip(part, bits)
        return pltpu.make_async_copy(
            wb.at[where, rows(part)], gathered.at[where, c, rows(part)], keep_sem.at[slot, part])

    for part in parts:
        eighth_copy(part).wait_recv()
        start, count = PART_START[part], min(PART_ROWS[part], SHARD - PART_START[part])
        pieces = [(start, count)] if count % 16 == 0 else [(start, count // 16 * 16), (start + count // 16 * 16, count % 16)]
        for first, size in pieces:
            span = pl.ds(first, size)
            grad_sum = (acc[here, span] + eighth[part, pl.ds(first - start, size)]) / DEVICES
            m_val = BETA_ONE * m_buf[span] + (1.0 - BETA_ONE) * grad_sum
            v_val = BETA_TWO * v_buf[span] + (1.0 - BETA_TWO) * grad_sum * grad_sum
            m_hat = m_val / (1.0 - BETA_ONE ** ADAM_STEP)
            v_hat = v_val / (1.0 - BETA_TWO ** ADAM_STEP)
            w_val = w_buf[span] - LEARN_RATE * m_hat / (jnp.sqrt(v_hat) + ADAM_EPS)
            m_buf[span] = m_val
            v_buf[span] = v_val
            w_buf[span] = w_val
            if size % 16:
                w_val = jnp.concatenate([w_val, jnp.zeros((16 - size % 16, LANES), jnp.float32)], axis=0)
                span = pl.ds(first, 16)
            wb[here, span] = w_val.astype(jnp.bfloat16)
        for hop in range(3):
            ring_copy((0, 0, 0), hop, part).start()
        share_copy((0, 0, 0), part).start()
        keep_copy((0, 0, 0), part).start()

    store = [
        pltpu.make_async_copy(m_buf, m_new, store_sem.at[0]),
        pltpu.make_async_copy(v_buf, v_new, store_sem.at[1]),
        pltpu.make_async_copy(w_buf, w_new, store_sem.at[2]),
    ]
    for copy in store:
        copy.start()

    def last_hop(bits):
        return max(n for n in range(3) if bits[n])

    for bits in GATHER_ORDER:
        hop = last_hop(bits)
        came = tuple(1 - bit if n == hop else bit for n, bit in enumerate(bits))
        for part in parts:
            ring_copy(came, hop, part).wait_recv()
            for later in range(hop + 1, 3):
                ring_copy(bits, later, part).start()
            share_copy(bits, part).start()
            keep_copy(bits, part).start()

    for n in range(8):
        for part in parts:
            pair_copy(n, part).wait_send()
    for part in parts:
        for k in range(4):
            half_copy(k, part).wait_send()
        for k in range(2):
            quarter_copy(k, part).wait_send()
        eighth_copy(part).wait_send()
        for bits in ((0, 0, 0),) + GATHER_ORDER:
            for later in range(0 if not any(bits) else last_hop(bits) + 1, 3):
                ring_copy(bits, later, part).wait_send()
            share_copy(bits, part).wait()
            keep_copy(bits, part).wait()
    for copy in store:
        copy.wait()


def exchange(grad, opt_m, opt_v, master):
    shape = jax.ShapeDtypeStruct
    state_shape = shape((SHARD, LANES), jnp.float32)
    f32 = functools.partial(pltpu.VMEM, dtype=jnp.float32)
    dma = pltpu.SemaphoreType.DMA
    scratch = [
        f32((8, PAD, LANES)), f32((8, PAD, LANES)),
        f32((3, 4, PART_MAX, LANES)), f32((3, 2, PART_MAX, LANES)), f32((3, PART_MAX, LANES)),
        f32((SHARD, LANES)), f32((SHARD, LANES)), f32((SHARD, LANES)),
        pltpu.VMEM((8, PAD, LANES), jnp.bfloat16),
        dma((8, 3)), dma((8, 3)), dma((8, 3)), dma((4, 3)), dma((4, 3)), dma((2, 3)), dma((2, 3)),
        dma((3,)), dma((3,)), dma((3,)), dma((3,)),
        dma((8, 3)), dma((8, 3)), dma((8, 3)), dma((8, 3)), dma((8, 3)),
    ]
    return pl.pallas_call(
        exchange_kernel,
        out_shape=(state_shape, state_shape, state_shape, shape((8, 2, PAD, LANES), jnp.bfloat16)),
        in_specs=[pl.BlockSpec(memory_space=pl.ANY)] * 4,
        out_specs=(pl.BlockSpec(memory_space=pl.ANY),) * 4,
        scratch_shapes=scratch,
        compiler_params=pltpu.CompilerParams(vmem_limit_bytes=VMEM_MAX, collective_id=0, has_side_effects=True),
        name="exchange",
    )(grad, opt_m, opt_v, master)


def unflatten_kernel(flat_in, o_emb, o_attn, o_in, o_out, halves, flat, b_emb, b_attn, b_in, b_out, in_sem, out_sem):
    outs = (o_emb, o_attn, o_in, o_out)
    bufs = (b_emb, b_attn, b_in, b_out)
    chunks = flat_chunks()

    def load(owner):
        return pltpu.make_async_copy(flat_in.at[owner], halves.at[owner], in_sem.at[owner])

    def put(k):
        index, start, step = chunks[k]
        return pltpu.make_async_copy(
            bufs[index].at[pl.ds(start, step)], outs[index].at[pl.ds(start, step)], out_sem.at[k])

    for owner in range(DEVICES):
        load(owner).start()
    ready = 0
    for k, (index, start, step) in enumerate(chunks):
        _, cols, base = TENSORS[index]
        groups = cols // LANES
        buf = bufs[index]
        need = base + (start + step) * groups
        while ready * SHARD < need:
            load(ready).wait()
            at = ready * SHARD
            whole = SHARD // 16

            def widen(t, carry, at=at, ready=ready):
                row = pl.multiple_of(t * 16, 16)
                flat[pl.ds(at + row, 16), :] = halves[ready, pl.ds(row, 16), :].astype(jnp.float32)
                return carry

            lax.fori_loop(0, whole, widen, 0, unroll=8)
            tail = halves[ready, whole * 16:whole * 16 + 16, :].astype(jnp.float32)
            flat[at + whole * 16:at + SHARD, :] = tail[:SHARD - whole * 16]
            ready = ready + 1

        def body(t, carry, base=base, groups=groups, buf=buf):
            row = pl.multiple_of(t * 16, 16)
            for j in range(groups):
                q = base + row * groups + j
                top = flat[pl.ds(q, 8, stride=groups), :]
                low = flat[pl.ds(q + 8 * groups, 8, stride=groups), :]
                buf[pl.ds(row, 16), j * LANES:(j + 1) * LANES] = (
                    jnp.concatenate([top, low], axis=0).astype(jnp.bfloat16))
            return carry

        lax.fori_loop(start // 16, (start + step) // 16, body, 0, unroll=2)
        put(k).start()
    for k in range(len(chunks)):
        put(k).wait()
    while ready < DEVICES:
        load(ready).wait()
        ready = ready + 1


def unflatten(flat):
    bf16 = jnp.bfloat16
    return pl.pallas_call(
        unflatten_kernel,
        out_shape=tuple(jax.ShapeDtypeStruct((rows, cols), bf16) for rows, cols, _ in TENSORS),
        in_specs=[pl.BlockSpec(memory_space=pl.ANY)],
        out_specs=(pl.BlockSpec(memory_space=pl.ANY),) * 4,
        scratch_shapes=[pltpu.VMEM((DEVICES, PAD, LANES), bf16), pltpu.VMEM((DEVICES * SHARD, LANES), jnp.float32)]
        + [pltpu.VMEM((rows, cols), bf16) for rows, cols, _ in TENSORS]
        + [pltpu.SemaphoreType.DMA((DEVICES,)), pltpu.SemaphoreType.DMA((len(flat_chunks()),))],
        compiler_params=pltpu.CompilerParams(vmem_limit_bytes=VMEM_MAX),
        name="unflatten",
    )(flat)


SUB = 256
BLOCK = 2048
COLS = 512
GELU_A = math.sqrt(2.0 / math.pi)
GELU_B = GELU_A * 0.044715


def ffn_kernel(ids, act, flat, w_in, b_in, w_out, b_out, y_out, table, rows_buf, h_buf, u_buf, halves, sem):
    step = pl.program_id(0)

    @pl.when(step == 0)
    def _():
        for owner in range(4):
            pltpu.make_async_copy(flat.at[owner], halves.at[owner], sem.at[owner]).start()
        for owner in range(4):
            pltpu.make_async_copy(flat.at[owner], halves.at[owner], sem.at[owner]).wait()
            at = owner * SHARD
            count = min(SHARD, VOCAB * D // LANES - at)
            whole = count // 16

            def widen(t, carry, at=at, owner=owner):
                row = pl.multiple_of(t * 16, 16)
                table[pl.ds(at + row, 16), :] = halves[owner, pl.ds(row, 16), :].astype(jnp.float32) * math.sqrt(D)
                return carry

            lax.fori_loop(0, whole, widen, 0, unroll=8)
            if count % 16:
                tail = halves[owner, whole * 16:whole * 16 + 16, :].astype(jnp.float32) * math.sqrt(D)
                table[at + whole * 16:at + count, :] = tail[:count - whole * 16]

    def sub_block(s, carry):
        first = pl.multiple_of(s * SUB, SUB)
        token = step * BLOCK + first
        for tile in range(SUB // 8):
            for i in range(8):
                row = ids[token + tile * 8 + i] * 6
                rows_buf[pl.ds(tile * 48 + i, 6, stride=8), :] = table[pl.ds(row, 6), :]
        for pair in range(SUB // 16):
            for j in range(6):
                top = rows_buf[pair * 96 + j * 8:pair * 96 + j * 8 + 8, :]
                low = rows_buf[pair * 96 + 48 + j * 8:pair * 96 + 48 + j * 8 + 8, :]
                both = jnp.concatenate([top, low], axis=0)
                a_val = act[pl.ds(first + pair * 16, 16), j * LANES:(j + 1) * LANES].astype(jnp.float32)
                h_buf[pair * 16:pair * 16 + 16, j * LANES:(j + 1) * LANES] = (both + a_val).astype(jnp.bfloat16)
        h_val = h_buf[...]
        for f in range(0, FF, COLS):
            pre = jnp.dot(h_val, w_in[:, f:f + COLS], preferred_element_type=jnp.float32) + b_in[:, f:f + COLS]
            bent = jnp.tanh(pre * (GELU_A + GELU_B * (pre * pre)))
            part = 0.5 * pre
            u_buf[:, f:f + COLS] = (part + part * bent).astype(jnp.bfloat16)
        y_val = jnp.dot(u_buf[...], w_out[...], preferred_element_type=jnp.float32) + b_out[...]
        y_out[pl.ds(first, SUB), :] = y_val.astype(jnp.bfloat16)
        return carry

    lax.fori_loop(0, BLOCK // SUB, sub_block, 0)


def ffn(ids, act, flat, w_in, b_in, w_out, b_out):
    tokens = act.shape[0]
    whole = lambda i, ids: (0, 0)
    grid_spec = pltpu.PrefetchScalarGridSpec(
        num_scalar_prefetch=1,
        grid=(tokens // BLOCK,),
        in_specs=[
            pl.BlockSpec((BLOCK, D), lambda i, ids: (i, 0)),
            pl.BlockSpec(memory_space=pl.ANY),
            pl.BlockSpec((D, FF), whole),
            pl.BlockSpec((1, FF), whole),
            pl.BlockSpec((FF, D), whole),
            pl.BlockSpec((1, D), whole),
        ],
        out_specs=pl.BlockSpec((BLOCK, D), lambda i, ids: (i, 0)),
        scratch_shapes=[
            pltpu.VMEM((VOCAB * D // LANES, LANES), jnp.float32),
            pltpu.VMEM((SUB * 6, LANES), jnp.float32),
            pltpu.VMEM((SUB, D), jnp.bfloat16),
            pltpu.VMEM((SUB, FF), jnp.bfloat16),
            pltpu.VMEM((4, PAD, LANES), jnp.bfloat16),
            pltpu.SemaphoreType.DMA((4,)),
        ],
    )
    return pl.pallas_call(
        ffn_kernel,
        out_shape=jax.ShapeDtypeStruct((tokens, D), jnp.bfloat16),
        grid_spec=grid_spec,
        compiler_params=pltpu.CompilerParams(vmem_limit_bytes=VMEM_MAX),
        name="ffn",
    )(ids, act, flat, w_in, b_in, w_out, b_out)


def solution(mesh):
    def device_step(g_emb, g_attn, g_in, g_out, g_vecd, g_vecf, opt_m, opt_v, master, tok_ids, act_in):
        vec = jnp.concatenate([
            g_vecd.reshape(-1, LANES), g_vecf.reshape(-1, LANES),
            jnp.zeros((VEC_ROWS - (9 * D + FF) // LANES, LANES), jnp.float32)], axis=0)
        grad = flatten(g_emb.reshape(VOCAB, D), g_attn.reshape(4 * D, D), g_in.reshape(D, FF), g_out.reshape(FF, D), vec)
        m_new, v_new, w_new, gathered = exchange(
            grad.reshape(8, 2, PAD, LANES), opt_m.reshape(SHARD, LANES),
            opt_v.reshape(SHARD, LANES), master.reshape(SHARD, LANES))
        flat = gathered.reshape(DEVICES, PAD, LANES)
        wb_emb, wb_attn, wb_in, wb_out = unflatten(flat)
        first = VEC_BASE - SHARD * (DEVICES - 1)
        wb_vecd = flat[DEVICES - 1, first:first + 9 * D // LANES].reshape(9, D)
        wb_vecf = flat[DEVICES - 1, first + 9 * D // LANES:first + (9 * D + FF) // LANES].reshape(1, FF)
        y_out = ffn(tok_ids, act_in, flat, wb_in, wb_vecf.astype(jnp.float32), wb_out,
                    wb_vecd[8:9].astype(jnp.float32))
        return (m_new.reshape(-1), v_new.reshape(-1), w_new.reshape(-1), wb_emb, wb_attn.reshape(1, 4, D, D),
                wb_in[None], wb_out[None], wb_vecd[None], wb_vecf, y_out)

    grad_specs = tuple(P(AXES, *([None] * (grad_rank - 1))) for grad_rank in GRAD_RANKS)
    in_specs = grad_specs + (P(AXES), P(AXES), P(AXES), P(AXES), P(AXES, None))
    out_specs = (P(AXES), P(AXES), P(AXES), P(), P(), P(), P(), P(), P(), P(AXES, None))
    return jax.shard_map(device_step, mesh=mesh, in_specs=in_specs, out_specs=out_specs, check_vma=False)
```

time: 1080 us -> 359 us (0.33)
  waiting for transfers between devices: 390 us -> 0 us
  Pallas kernels: 0 us -> 346 us
  other arithmetic: 303 us -> 3.5 us
  local copies, waits for them, and re-layouts: 212 us -> 8.45 us
  matrix products: 157 us -> 0 us
  between operations: 14.4 us -> 0.71 us
    pallas_call x0 -> x4, Pallas kernels: none -> 346 us  [the longest x1 163 us: ffn(): pl.pallas_call(ffn_kernel, out_shape=jax.ShapeDtypeStruct((tokens, D), jn...]
    all_gather x1 -> x0, other arithmetic: 293 us -> none  [device_step(): lax.all_gather(w_new.astype(jnp.bfloat16), AXES, axis=0, tiled=True)]
    unnamed x3 -> x0, waiting for transfers between devices: 277 us -> none
    dot_general x2 -> x0, matrix products: 157 us -> none  [the longest x1 95.7 us: ffn_block(): jnp.dot(hidden, w_in, preferred_element_type=jnp.float32)]
    all_gather x1 -> x0, waiting for transfers between devices: 112 us -> none  [device_step(): lax.all_gather(w_new.astype(jnp.bfloat16), AXES, axis=0, tiled=True)]
    gather x1 -> x0, local copies, waits for them, and re-layouts: 67.8 us -> none  [ffn_block(): emb_rows = jnp.take(wb_emb, tok_ids, axis=0).astype(jnp.float32)]
    unnamed x28 -> x9, local copies, waits for them, and re-layouts: 63.3 us -> 6.87 us
    reshape x10 -> x1, local copies, waits for them, and re-layouts: 49.5 us -> 0.01 us  [device_step(): g_vecd.reshape(-1, LANES)]
  transfers between devices with their start and end apart: 2 -> 0, of which waited for: 2 -> 0; matrix products, arithmetic and copies ran while one was open for 0% -> 0% of each run, Pallas kernels for 0% -> 0%
where the time goes in v1:
time: 359 us; the launch traced here: 358 us
  Pallas kernels  346 us (96%)
  local copies, waits for them, and re-layouts  8.45 us (2%)
    pallas_call x1, Pallas kernels, ffn(): pl.pallas_call(ffn_kernel, out_shape=jax.ShapeDtypeStruct((tokens, D), jn...  163 us
    pallas_call x1, Pallas kernels, exchange(): pl.pallas_call(exchange_kernel, out_shape=(state_shape, state_shape, stat...  149 us
    pallas_call x1, Pallas kernels, flatten(): pl.pallas_call(flatten_kernel, out_shape=jax.ShapeDtypeStruct((DEVICES, P...  19.6 us
    pallas_call x1, Pallas kernels, unflatten(): pl.pallas_call(unflatten_kernel, out_shape=tuple((jax.ShapeDtypeStruct((r...  13.3 us

profile of v1, /device:TPU:0, one launch (start us, length us, event | category | flops | bytes accessed | tf_op | source)
XLA Modules:
  0.0 358.4 jit_solution(17998586535801259089)
XLA Ops:
  0.6 0.8 reduce
  1.5 0.1 pad.2.clone
  1.6 1.4 maximum_maximum_fusion.vec
  3.0 19.6 %flatten.1 = f32[16,3472,128]{2,1,0:T(8,128)} custom-call(f32[2048,768]{1,0:T(8,128)} %bitcast.33, f32[3072,768]{1,0:T(8,128)} %bitcast.32, f32[768,2048]{1,0:T(8,128)} %bitcast.34, f32[2048,768]{1,0:T(8,128)} %bitcast.35, f32[80,128]{1,0:T(8,128)} %maximum_maximum_fusion.vec), custom_call_target="tpu_custom_call" | custom-call | tf_op jit(solution)/shard_map/flatten/pallas_call | solution.py:124
  22.6 149.5 %exchange.1 = (f32[3461,128]{1,0:T(8,128)}, f32[3461,128]{1,0:T(8,128)}, f32[3461,128]{1,0:T(8,128)}, bf16[8,2,3472,128]{3,2,1,0:T(8,128)(2,1)}) custom-call(f32[8,2,3472,128]{3,2,1,0:T(8,128)} %bitcast.26, f32[3461,128]{1,0:T(8,128)} %bitcast.38, f32[3461,128]{1,0:T(8,128)} %bitcast.39, f32[3461,128]{1,0:T(8,128)} %bitcast.40), custom_call_target="tpu_custom_call" | custom-call | tf_op jit(solution)/shard_map/exchange/pallas_call | solution.py:347
  172.1 13.3 %unflatten.1 = (bf16[2048,768]{1,0:T(8,128)(2,1)}, bf16[3072,768]{1,0:T(8,128)(2,1)}, bf16[768,2048]{1,0:T(8,128)(2,1)}, bf16[2048,768]{1,0:T(8,128)(2,1)}) custom-call(bf16[16,3472,128]{2,1,0:T(8,128)(2,1)} %bitcast.27), custom_call_target="tpu_custom_call" | custom-call | tf_op jit(solution)/shard_map/unflatten/pallas_call | solution.py:415
  185.4 0.7 slice_bitcast_fusion
  186.1 0.6 fusion
  186.7 0.7 convert_bitcast_fusion
  187.4 0.6 copy.26
  188.0 163.4 %ffn.1 = bf16[16384,768]{1,0:T(8,128)(2,1)} custom-call(s32[16384]{0:T(1024)} %ids.1, bf16[16384,768]{1,0:T(8,128)(2,1)} %act.1, bf16[16,3472,128]{2,1,0:T(8,128)(2,1)} %bitcast.30, bf16[768,2048]{1,0:T(8,128)(2,1)} %get-tuple-element.24.w_in, f32[1,2048]{1,0:T(1,128)} %get-tuple-element.26.b_in, bf16[2048,768]{1,0:T(8,128)(2,1)} %get-tuple-element.25.w_out, ...), custom_call_target="tpu_custom_call" | custom-call | tf_op jit(solution)/shard_map/ffn/pallas_call | solution.py:509
  351.3 0.0 copy-start.1
  351.4 0.9 slice.14
  352.2 0.6 broadcast_in_dim_reshape_squeeze.3
  352.9 0.0 copy-start
  352.9 2.9 copy.30
  355.8 0.0 copy-done.1
  355.8 1.3 copy.31
  357.1 0.0 copy-done
  357.1 1.3 copy.32
  (2 shorter events, 0.0 us)
Async XLA Ops:
  351.3 4.4 %copy-start.1 = (f32[3461,128]{1,0:T(8,128)S(1)}, f32[3461,128]{1,0:T(8,128)}, u32[]{:S(2)}) copy-start(f32[3461,128]{1,0:T(8,128)} %get-tuple-element.19) | copy-start | bytes 5316100
  352.9 4.3 %copy-start = (f32[3461,128]{1,0:T(8,128)S(1)}, f32[3461,128]{1,0:T(8,128)}, u32[]{:S(2)}) copy-start(f32[3461,128]{1,0:T(8,128)} %get-tuple-element.20) | copy-start | bytes 5316100

commit v2 on v1

--- a/solution.py
+++ b/solution.py
@@ -355,164 +355,218 @@
     )(grad, opt_m, opt_v, master)
 
 
-def unflatten_kernel(flat_in, o_emb, o_attn, o_in, o_out, halves, flat, b_emb, b_attn, b_in, b_out, in_sem, out_sem):
-    outs = (o_emb, o_attn, o_in, o_out)
-    bufs = (b_emb, b_attn, b_in, b_out)
-    chunks = flat_chunks()
-
-    def load(owner):
-        return pltpu.make_async_copy(flat_in.at[owner], halves.at[owner], in_sem.at[owner])
-
-    def put(k):
-        index, start, step = chunks[k]
-        return pltpu.make_async_copy(
-            bufs[index].at[pl.ds(start, step)], outs[index].at[pl.ds(start, step)], out_sem.at[k])
-
-    for owner in range(DEVICES):
-        load(owner).start()
-    ready = 0
-    for k, (index, start, step) in enumerate(chunks):
-        _, cols, base = TENSORS[index]
-        groups = cols // LANES
-        buf = bufs[index]
-        need = base + (start + step) * groups
-        while ready * SHARD < need:
-            load(ready).wait()
-            at = ready * SHARD
-            whole = SHARD // 16
-
-            def widen(t, carry, at=at, ready=ready):
-                row = pl.multiple_of(t * 16, 16)
-                flat[pl.ds(at + row, 16), :] = halves[ready, pl.ds(row, 16), :].astype(jnp.float32)
-                return carry
-
-            lax.fori_loop(0, whole, widen, 0, unroll=8)
-            tail = halves[ready, whole * 16:whole * 16 + 16, :].astype(jnp.float32)
-            flat[at + whole * 16:at + SHARD, :] = tail[:SHARD - whole * 16]
-            ready = ready + 1
-
-        def body(t, carry, base=base, groups=groups, buf=buf):
-            row = pl.multiple_of(t * 16, 16)
-            for j in range(groups):
-                q = base + row * groups + j
-                top = flat[pl.ds(q, 8, stride=groups), :]
-                low = flat[pl.ds(q + 8 * groups, 8, stride=groups), :]
-                buf[pl.ds(row, 16), j * LANES:(j + 1) * LANES] = (
-                    jnp.concatenate([top, low], axis=0).astype(jnp.bfloat16))
-            return carry
-
-        lax.fori_loop(start // 16, (start + step) // 16, body, 0, unroll=2)
-        put(k).start()
-    for k in range(len(chunks)):
-        put(k).wait()
-    while ready < DEVICES:
-        load(ready).wait()
-        ready = ready + 1
-
-
-def unflatten(flat):
-    bf16 = jnp.bfloat16
-    return pl.pallas_call(
-        unflatten_kernel,
-        out_shape=tuple(jax.ShapeDtypeStruct((rows, cols), bf16) for rows, cols, _ in TENSORS),
-        in_specs=[pl.BlockSpec(memory_space=pl.ANY)],
-        out_specs=(pl.BlockSpec(memory_space=pl.ANY),) * 4,
-        scratch_shapes=[pltpu.VMEM((DEVICES, PAD, LANES), bf16), pltpu.VMEM((DEVICES * SHARD, LANES), jnp.float32)]
-        + [pltpu.VMEM((rows, cols), bf16) for rows, cols, _ in TENSORS]
-        + [pltpu.SemaphoreType.DMA((DEVICES,)), pltpu.SemaphoreType.DMA((len(flat_chunks()),))],
-        compiler_params=pltpu.CompilerParams(vmem_limit_bytes=VMEM_MAX),
-        name="unflatten",
-    )(flat)
-
-
-SUB = 256
-BLOCK = 2048
-COLS = 512
+SUB = 512
+CHUNK = 2 * SUB
+RING = 6
+ACT_SLOTS = 3
 GELU_A = math.sqrt(2.0 / math.pi)
 GELU_B = GELU_A * 0.044715
-
-
-def ffn_kernel(ids, act, flat, w_in, b_in, w_out, b_out, y_out, table, rows_buf, h_buf, u_buf, halves, sem):
-    step = pl.program_id(0)
-
-    @pl.when(step == 0)
-    def _():
-        for owner in range(4):
-            pltpu.make_async_copy(flat.at[owner], halves.at[owner], sem.at[owner]).start()
-        for owner in range(4):
-            pltpu.make_async_copy(flat.at[owner], halves.at[owner], sem.at[owner]).wait()
-            at = owner * SHARD
-            count = min(SHARD, VOCAB * D // LANES - at)
-            whole = count // 16
-
-            def widen(t, carry, at=at, owner=owner):
+WIDEN_ORDER = (8, 9, 10, 11, 12, 13, 14, 15, 0, 1, 2, 3, 4, 5, 6, 7)
+
+
+def ffn_kernel(steps, ids, act, flat, m_in, v_in, master_in,
+               y_out, o_emb, o_attn, o_in, o_out, o_vecd, o_vecf, m_out, v_out, master_out,
+               dense, ring, act_buf, y_buf, w_in, w_out, b_in, b_out, vecd_wide, vecd_buf, vecf_buf,
+               rows_one, rows_two, h_one, h_two, u_one, u_two, emb_buf, attn_buf, state_buf,
+               ring_sem, act_sem, y_sem, emb_sem, attn_sem, weight_sem, state_sem):
+    emb_rows, attn_rows = VOCAB // steps, 4 * D // steps
+
+    def load_act(it):
+        return pltpu.make_async_copy(
+            act.at[pl.ds(it * CHUNK, CHUNK)], act_buf.at[lax.rem(it, ACT_SLOTS)], act_sem.at[lax.rem(it, ACT_SLOTS)])
+
+    def store_y(it):
+        return pltpu.make_async_copy(
+            y_buf.at[lax.rem(it, 2)], y_out.at[pl.ds(it * CHUNK, CHUNK)], y_sem.at[lax.rem(it, 2)])
+
+    def store_emb(it):
+        return pltpu.make_async_copy(
+            emb_buf.at[lax.rem(it, 2)], o_emb.at[pl.ds(it * emb_rows, emb_rows)], emb_sem.at[lax.rem(it, 2)])
+
+    def store_attn(it):
+        return pltpu.make_async_copy(
+            attn_buf.at[lax.rem(it, 2)], o_attn.at[pl.ds(it * attn_rows, attn_rows)], attn_sem.at[lax.rem(it, 2)])
+
+    def load_flat(n):
+        return pltpu.make_async_copy(flat.at[WIDEN_ORDER[n]], ring.at[n % RING], ring_sem.at[n % RING])
+
+    for n in range(RING):
+        load_flat(n).start()
+    load_act(0).start()
+    load_act(1).start()
+
+    def relayout(base, groups, row, buf, at):
+        for j in range(groups):
+            q = base + row * groups + j
+            top = dense[pl.ds(q, 8, stride=groups), :]
+            low = dense[pl.ds(q + 8 * groups, 8, stride=groups), :]
+            buf[pl.ds(at, 16), j * LANES:(j + 1) * LANES] = jnp.concatenate([top, low], axis=0).astype(jnp.bfloat16)
+
+    for n, owner in enumerate(WIDEN_ORDER):
+        load_flat(n).wait()
+        at = owner * SHARD
+        whole = SHARD // 16
+
+        def widen(t, carry, at=at, slot=n % RING):
+            row = pl.multiple_of(t * 16, 16)
+            dense[pl.ds(at + row, 16), :] = ring[slot, pl.ds(row, 16), :].astype(jnp.float32)
+            return carry
+
+        lax.fori_loop(0, whole, widen, 0, unroll=24)
+        tail = ring[n % RING, whole * 16:whole * 16 + 16, :].astype(jnp.float32)
+        dense[at + whole * 16:at + SHARD, :] = tail[:SHARD - whole * 16]
+        if n + RING < DEVICES:
+            load_flat(n + RING).start()
+        if owner == 12:
+            def fill_in(t, carry):
                 row = pl.multiple_of(t * 16, 16)
-                table[pl.ds(at + row, 16), :] = halves[owner, pl.ds(row, 16), :].astype(jnp.float32) * math.sqrt(D)
+                relayout(TENSORS[2][2], FF // LANES, row, w_in, row)
                 return carry
 
-            lax.fori_loop(0, whole, widen, 0, unroll=8)
-            if count % 16:
-                tail = halves[owner, whole * 16:whole * 16 + 16, :].astype(jnp.float32) * math.sqrt(D)
-                table[at + whole * 16:at + count, :] = tail[:count - whole * 16]
-
-    def sub_block(s, carry):
-        first = pl.multiple_of(s * SUB, SUB)
-        token = step * BLOCK + first
+            lax.fori_loop(0, D // 16, fill_in, 0, unroll=2)
+            pltpu.make_async_copy(w_in, o_in, weight_sem.at[0]).start()
+        if owner == 15:
+            def fill_out(t, carry):
+                row = pl.multiple_of(t * 16, 16)
+                relayout(TENSORS[3][2], D // LANES, row, w_out, row)
+                return carry
+
+            lax.fori_loop(0, FF // 16, fill_out, 0, unroll=4)
+            pltpu.make_async_copy(w_out, o_out, weight_sem.at[1]).start()
+            for i in range(9):
+                for j in range(D // LANES):
+                    q = VEC_BASE + i * (D // LANES) + j
+                    vecd_wide[i:i + 1, j * LANES:(j + 1) * LANES] = dense[q:q + 1, :]
+            for j in range(D // LANES):
+                q = VEC_BASE + 8 * (D // LANES) + j
+                b_out[:, j * LANES:(j + 1) * LANES] = dense[q:q + 1, :]
+            for j in range(FF // LANES):
+                q = VEC_BASE + 9 * (D // LANES) + j
+                b_in[:, j * LANES:(j + 1) * LANES] = dense[q:q + 1, :]
+            vecd_buf[...] = vecd_wide[...].astype(jnp.bfloat16)
+            vecf_buf[...] = b_in[...].astype(jnp.bfloat16)
+            pltpu.make_async_copy(vecd_buf, o_vecd, weight_sem.at[2]).start()
+            pltpu.make_async_copy(vecf_buf, o_vecf, weight_sem.at[3]).start()
+
+    def lookup(it, half, h_buf, rows_buf):
+        slot = lax.rem(it, ACT_SLOTS)
+        token = jnp.minimum(it, steps - 1) * CHUNK + half * SUB
         for tile in range(SUB // 8):
             for i in range(8):
-                row = ids[token + tile * 8 + i] * 6
-                rows_buf[pl.ds(tile * 48 + i, 6, stride=8), :] = table[pl.ds(row, 6), :]
+                row = ids[token + tile * 8 + i] * (D // LANES)
+                rows_buf[pl.ds(tile * 56 + i * 7, 8), :] = dense[pl.ds(row, 8), :]
         for pair in range(SUB // 16):
-            for j in range(6):
-                top = rows_buf[pair * 96 + j * 8:pair * 96 + j * 8 + 8, :]
-                low = rows_buf[pair * 96 + 48 + j * 8:pair * 96 + 48 + j * 8 + 8, :]
-                both = jnp.concatenate([top, low], axis=0)
-                a_val = act[pl.ds(first + pair * 16, 16), j * LANES:(j + 1) * LANES].astype(jnp.float32)
+            for j in range(D // LANES):
+                top = rows_buf[pl.ds(pair * 112 + j, 8, stride=7), :]
+                low = rows_buf[pl.ds(pair * 112 + 56 + j, 8, stride=7), :]
+                both = jnp.concatenate([top, low], axis=0) * math.sqrt(D)
+                first = half * SUB + pair * 16
+                a_val = act_buf[slot, first:first + 16, j * LANES:(j + 1) * LANES].astype(jnp.float32)
                 h_buf[pair * 16:pair * 16 + 16, j * LANES:(j + 1) * LANES] = (both + a_val).astype(jnp.bfloat16)
-        h_val = h_buf[...]
-        for f in range(0, FF, COLS):
-            pre = jnp.dot(h_val, w_in[:, f:f + COLS], preferred_element_type=jnp.float32) + b_in[:, f:f + COLS]
-            bent = jnp.tanh(pre * (GELU_A + GELU_B * (pre * pre)))
-            part = 0.5 * pre
-            u_buf[:, f:f + COLS] = (part + part * bent).astype(jnp.bfloat16)
+
+    def multiply(it, half, h_buf, u_buf):
+        pre = jnp.dot(h_buf[...], w_in[...], preferred_element_type=jnp.float32) + b_in[...]
+        bent = jnp.tanh(pre * (GELU_A + GELU_B * (pre * pre)))
+        part = 0.5 * pre
+        u_buf[...] = (part + part * bent).astype(jnp.bfloat16)
         y_val = jnp.dot(u_buf[...], w_out[...], preferred_element_type=jnp.float32) + b_out[...]
-        y_out[pl.ds(first, SUB), :] = y_val.astype(jnp.bfloat16)
+        y_buf[lax.rem(it, 2), half * SUB:half * SUB + SUB, :] = y_val.astype(jnp.bfloat16)
+
+    load_act(0).wait()
+    lookup(0, 0, h_one, rows_one)
+
+    moves = []
+    for n, (source, target) in enumerate(((m_in, m_out), (v_in, v_out), (master_in, master_out))):
+        moves.append(pltpu.make_async_copy(source, state_buf, state_sem.at[2 * n]))
+        moves.append(pltpu.make_async_copy(state_buf, target, state_sem.at[2 * n + 1]))
+
+    def body(it, carry):
+        @pl.when(it + 1 < steps)
+        def _():
+            load_act(it + 1).wait()
+
+        @pl.when(it + 2 < steps)
+        def _():
+            load_act(it + 2).start()
+
+        @pl.when(it >= 2)
+        def _():
+            store_y(it - 2).wait()
+            store_emb(it - 2).wait()
+            store_attn(it - 2).wait()
+
+        for n, move in enumerate(moves):
+            @pl.when(it == 1 + 2 * n)
+            def _(n=n, move=move):
+                if n:
+                    moves[n - 1].wait()
+                move.start()
+
+        lookup(it, 1, h_two, rows_two)
+        multiply(it, 0, h_one, u_one)
+        lookup(it + 1, 0, h_one, rows_one)
+        multiply(it, 1, h_two, u_two)
+        for t in range(emb_rows // 16):
+            relayout(TENSORS[0][2], D // LANES, it * emb_rows + t * 16, emb_buf.at[lax.rem(it, 2)], t * 16)
+        for t in range(attn_rows // 16):
+            relayout(TENSORS[1][2], D // LANES, it * attn_rows + t * 16, attn_buf.at[lax.rem(it, 2)], t * 16)
+        store_y(it).start()
+        store_emb(it).start()
+        store_attn(it).start()
         return carry
 
-    lax.fori_loop(0, BLOCK // SUB, sub_block, 0)
-
-
-def ffn(ids, act, flat, w_in, b_in, w_out, b_out):
+    lax.fori_loop(0, steps, body, 0)
+    for it in (steps - 2, steps - 1):
+        store_y(it).wait()
+        store_emb(it).wait()
+        store_attn(it).wait()
+    moves[-1].wait()
+    pltpu.make_async_copy(w_in, o_in, weight_sem.at[0]).wait()
+    pltpu.make_async_copy(w_out, o_out, weight_sem.at[1]).wait()
+    pltpu.make_async_copy(vecd_buf, o_vecd, weight_sem.at[2]).wait()
+    pltpu.make_async_copy(vecf_buf, o_vecf, weight_sem.at[3]).wait()
+
+
+def ffn(ids, act, flat, m_new, v_new, w_new):
     tokens = act.shape[0]
-    whole = lambda i, ids: (0, 0)
-    grid_spec = pltpu.PrefetchScalarGridSpec(
-        num_scalar_prefetch=1,
-        grid=(tokens // BLOCK,),
-        in_specs=[
-            pl.BlockSpec((BLOCK, D), lambda i, ids: (i, 0)),
-            pl.BlockSpec(memory_space=pl.ANY),
-            pl.BlockSpec((D, FF), whole),
-            pl.BlockSpec((1, FF), whole),
-            pl.BlockSpec((FF, D), whole),
-            pl.BlockSpec((1, D), whole),
+    steps = tokens // CHUNK
+    f32, bf16 = jnp.float32, jnp.bfloat16
+    shape = jax.ShapeDtypeStruct
+    dma = pltpu.SemaphoreType.DMA
+    anywhere = pl.BlockSpec(memory_space=pl.ANY)
+    state = shape((SHARD, LANES), f32)
+    return pl.pallas_call(
+        functools.partial(ffn_kernel, steps),
+        out_shape=(shape((tokens, D), bf16), shape((VOCAB, D), bf16), shape((4 * D, D), bf16), shape((D, FF), bf16),
+                   shape((FF, D), bf16), shape((9, D), bf16), shape((1, FF), bf16), state, state, state),
+        in_specs=[pl.BlockSpec(memory_space=pltpu.SMEM)] + [anywhere] * 5,
+        out_specs=(anywhere,) * 10,
+        scratch_shapes=[
+            pltpu.VMEM((DEVICES * SHARD, LANES), f32),
+            pltpu.VMEM((RING, PAD, LANES), bf16),
+            pltpu.VMEM((ACT_SLOTS, CHUNK, D), bf16),
+            pltpu.VMEM((2, CHUNK, D), bf16),
+            pltpu.VMEM((D, FF), bf16),
+            pltpu.VMEM((FF, D), bf16),
+            pltpu.VMEM((1, FF), f32),
+            pltpu.VMEM((1, D), f32),
+            pltpu.VMEM((9, D), f32),
+            pltpu.VMEM((9, D), bf16),
+            pltpu.VMEM((1, FF), bf16),
+            pltpu.VMEM((SUB * 7 + 8, LANES), f32),
+            pltpu.VMEM((SUB * 7 + 8, LANES), f32),
+            pltpu.VMEM((SUB, D), bf16),
+            pltpu.VMEM((SUB, D), bf16),
+            pltpu.VMEM((SUB, FF), bf16),
+            pltpu.VMEM((SUB, FF), bf16),
+            pltpu.VMEM((2, VOCAB // steps, D), bf16),
+            pltpu.VMEM((2, 4 * D // steps, D), bf16),
+            pltpu.VMEM((SHARD, LANES), f32),
+            dma((RING,)), dma((ACT_SLOTS,)), dma((2,)), dma((2,)), dma((2,)), dma((4,)), dma((6,)),
         ],
-        out_specs=pl.BlockSpec((BLOCK, D), lambda i, ids: (i, 0)),
-        scratch_shapes=[
-            pltpu.VMEM((VOCAB * D // LANES, LANES), jnp.float32),
-            pltpu.VMEM((SUB * 6, LANES), jnp.float32),
-            pltpu.VMEM((SUB, D), jnp.bfloat16),
-            pltpu.VMEM((SUB, FF), jnp.bfloat16),
-            pltpu.VMEM((4, PAD, LANES), jnp.bfloat16),
-            pltpu.SemaphoreType.DMA((4,)),
-        ],
-    )
-    return pl.pallas_call(
-        ffn_kernel,
-        out_shape=jax.ShapeDtypeStruct((tokens, D), jnp.bfloat16),
-        grid_spec=grid_spec,
         compiler_params=pltpu.CompilerParams(vmem_limit_bytes=VMEM_MAX),
         name="ffn",
-    )(ids, act, flat, w_in, b_in, w_out, b_out)
+    )(ids, act, flat, m_new, v_new, w_new)
 
 
 def solution(mesh):
@@ -525,12 +579,8 @@
             grad.reshape(8, 2, PAD, LANES), opt_m.reshape(SHARD, LANES),
             opt_v.reshape(SHARD, LANES), master.reshape(SHARD, LANES))
         flat = gathered.reshape(DEVICES, PAD, LANES)
-        wb_emb, wb_attn, wb_in, wb_out = unflatten(flat)
-        first = VEC_BASE - SHARD * (DEVICES - 1)
-        wb_vecd = flat[DEVICES - 1, first:first + 9 * D // LANES].reshape(9, D)
-        wb_vecf = flat[DEVICES - 1, first + 9 * D // LANES:first + (9 * D + FF) // LANES].reshape(1, FF)
-        y_out = ffn(tok_ids, act_in, flat, wb_in, wb_vecf.astype(jnp.float32), wb_out,
-                    wb_vecd[8:9].astype(jnp.float32))
+        y_out, wb_emb, wb_attn, wb_in, wb_out, wb_vecd, wb_vecf, m_new, v_new, w_new = ffn(
+            tok_ids, act_in, flat, m_new, v_new, w_new)
         return (m_new.reshape(-1), v_new.reshape(-1), w_new.reshape(-1), wb_emb, wb_attn.reshape(1, 4, D, D),
                 wb_in[None], wb_out[None], wb_vecd[None], wb_vecf, y_out)
 

time: 359 us -> 317 us (0.88)
  Pallas kernels: 346 us -> 313 us
  local copies, waits for them, and re-layouts: 8.45 us -> 0.08 us
    pallas_call x2 -> x1, Pallas kernels: 177 us -> 144 us  [ffn(): pl.pallas_call(functools.partial(ffn_kernel, steps), out_shape=(shape((to...]
    unnamed x9 -> x0, local copies, waits for them, and re-layouts: 6.87 us -> none
where the time goes in v2:
time: 317 us; the launch traced here: 316 us
  Pallas kernels  313 us (99%)
    pallas_call x1, Pallas kernels, exchange(): pl.pallas_call(exchange_kernel, out_shape=(state_shape, state_shape, stat...  149 us
    pallas_call x1, Pallas kernels, ffn(): pl.pallas_call(functools.partial(ffn_kernel, steps), out_shape=(shape((to...  144 us
    pallas_call x1, Pallas kernels, flatten(): pl.pallas_call(flatten_kernel, out_shape=jax.ShapeDtypeStruct((DEVICES, P...  19.6 us

profile of v2, /device:TPU:0, one launch (start us, length us, event | category | flops | bytes accessed | tf_op | source)
XLA Modules:
  0.0 316.2 jit_solution(10142104886151417117)
XLA Ops:
  0.7 0.1 pad.2.clone
  0.7 0.8 reduce
  1.6 1.4 maximum_maximum_fusion.vec
  3.0 19.6 %flatten.1 = f32[16,3472,128]{2,1,0:T(8,128)} custom-call(f32[2048,768]{1,0:T(8,128)} %bitcast.20, f32[3072,768]{1,0:T(8,128)} %bitcast.19, f32[768,2048]{1,0:T(8,128)} %bitcast.21, f32[2048,768]{1,0:T(8,128)} %bitcast.22, f32[80,128]{1,0:T(8,128)} %maximum_maximum_fusion.vec), custom_call_target="tpu_custom_call" | custom-call | tf_op jit(solution)/shard_map/flatten/pallas_call | solution.py:124
  22.6 149.5 %exchange.1 = (f32[3461,128]{1,0:T(8,128)}, f32[3461,128]{1,0:T(8,128)}, f32[3461,128]{1,0:T(8,128)}, bf16[8,2,3472,128]{3,2,1,0:T(8,128)(2,1)}) custom-call(f32[8,2,3472,128]{3,2,1,0:T(8,128)} %bitcast.17, f32[3461,128]{1,0:T(8,128)} %bitcast.23, f32[3461,128]{1,0:T(8,128)} %bitcast.24, f32[3461,128]{1,0:T(8,128)} %bitcast.25), custom_call_target="tpu_custom_call" | custom-call | tf_op jit(solution)/shard_map/exchange/pallas_call | solution.py:347
  172.1 144.0 %ffn.1 = (bf16[16384,768]{1,0:T(8,128)(2,1)}, bf16[2048,768]{1,0:T(8,128)(2,1)}, bf16[3072,768]{1,0:T(8,128)(2,1)}, bf16[768,2048]{1,0:T(8,128)(2,1)}, bf16[2048...) custom-call(s32[16384]{0:T(1024)} %ids.1, ...), custom_call_target="tpu_custom_call" | custom-call | tf_op jit(solution)/shard_map/ffn/pallas_call | solution.py:538
  (2 shorter events, 0.0 us)

commit v3 on v2

--- a/solution.py
+++ b/solution.py
@@ -35,112 +35,27 @@
     (D, FF, (VOCAB * D + 4 * D * D) // LANES),
     (FF, D, (VOCAB * D + 4 * D * D + D * FF) // LANES),
 )
+TILES = 48
+FLAT_ROWS = 8 * TILES
+CHUNKS = 144
+SPAN = 11
+MARGIN = FLAT_ROWS
+SLOT = 2 * MARGIN + 3464
+STAGES = 4
 VEC_BASE = (VOCAB * D + 4 * D * D + 2 * D * FF) // LANES
 VEC_ROWS = DEVICES * SHARD - VEC_BASE
 
 
-def flat_chunks():
-    chunks = []
-    for index, (rows, cols, base) in enumerate(TENSORS):
-        step = 256 if cols == D else 128
-        for start in range(0, rows, step):
-            chunks.append((index, start, step))
-    return chunks
-
-
-def flatten_kernel(g_emb, g_attn, g_in, g_out, vec, flat_out, s_emb, s_attn, s_in, s_out, s_vec, flat, in_sem, out_sem):
-    sources = (g_emb, g_attn, g_in, g_out)
-    stages = (s_emb, s_attn, s_in, s_out)
-    chunks = flat_chunks()
-
-    def load(k):
-        index, start, step = chunks[k]
-        return pltpu.make_async_copy(
-            sources[index].at[pl.ds(start, step)], stages[index].at[pl.ds(start, step)], in_sem.at[k])
-
-    vec_load = pltpu.make_async_copy(vec, s_vec, in_sem.at[len(chunks)])
-    for k in range(len(chunks)):
-        load(k).start()
-    vec_load.start()
-
-    def put(owner):
-        return pltpu.make_async_copy(flat.at[pl.ds(owner * PAD, PAD)], flat_out.at[owner], out_sem.at[owner])
-
-    sent = 0
-    for k, (index, start, step) in enumerate(chunks):
-        _, cols, base = TENSORS[index]
-        groups = cols // LANES
-        stage = stages[index]
-        load(k).wait()
-        tile = start // 8
-        last = (start + step) // 8
-        while tile < last:
-            first_row = base + tile * 8 * groups
-            owner = first_row // SHARD
-            fit = (SHARD * (owner + 1) - first_row) // (8 * groups)
-            run = min(fit, last - tile)
-            if run > 0:
-                shift = base + (PAD - SHARD) * owner
-
-                def body(t, carry, shift=shift, groups=groups, stage=stage):
-                    row = pl.multiple_of(t * 8, 8)
-                    for j in range(groups):
-                        flat[pl.ds(shift + row * groups + j, 8, stride=groups), :] = (
-                            stage[pl.ds(row, 8), j * LANES:(j + 1) * LANES])
-                    return carry
-
-                lax.fori_loop(tile, tile + run, body, 0, unroll=2)
-                tile = tile + run
-            else:
-                for i in range(8):
-                    for j in range(groups):
-                        q = first_row + i * groups + j
-                        p = q + (PAD - SHARD) * (q // SHARD)
-                        flat[p:p + 1, :] = stage[tile * 8 + i:tile * 8 + i + 1, j * LANES:(j + 1) * LANES]
-                tile = tile + 1
-        done = (base + last * 8 * groups) // SHARD
-        while sent < min(done, DEVICES - 1):
-            put(sent).start()
-            sent = sent + 1
-    vec_load.wait()
-    last_row = VEC_BASE + (PAD - SHARD) * (DEVICES - 1)
-    flat[last_row:last_row + VEC_ROWS, :] = s_vec[...]
-    while sent < DEVICES:
-        put(sent).start()
-        sent = sent + 1
-    for owner in range(DEVICES):
-        put(owner).wait()
-
-
-def flatten(g_emb, g_attn, g_in, g_out, vec):
-    chunk_count = len(flat_chunks())
-    scratch = [pltpu.VMEM((rows, cols), jnp.float32) for rows, cols, _ in TENSORS]
-    scratch += [
-        pltpu.VMEM((VEC_ROWS, LANES), jnp.float32),
-        pltpu.VMEM((DEVICES * PAD, LANES), jnp.float32),
-        pltpu.SemaphoreType.DMA((chunk_count + 1,)),
-        pltpu.SemaphoreType.DMA((DEVICES,)),
-    ]
-    return pl.pallas_call(
-        flatten_kernel,
-        out_shape=jax.ShapeDtypeStruct((DEVICES, PAD, LANES), jnp.float32),
-        in_specs=[pl.BlockSpec(memory_space=pl.ANY)] * 5,
-        out_specs=pl.BlockSpec(memory_space=pl.ANY),
-        scratch_shapes=scratch,
-        compiler_params=pltpu.CompilerParams(vmem_limit_bytes=VMEM_MAX),
-        name="flatten",
-    )(g_emb, g_attn, g_in, g_out, vec)
-
-
 ORDERS = (("x", "y", "z"), ("y", "z", "x"), ("z", "x", "y"))
 WEIGHT = {"z": 4, "y": 2, "x": 1}
+CHIP_ORDER = ("xyz", "xy", "yz", "zx", "x", "y", "z", "")
 HALF_ORDER = ((1, 1), (1, 0), (0, 1), (0, 0))
 GATHER_ORDER = ((1, 0, 0), (0, 1, 0), (0, 0, 1), (1, 1, 0), (1, 0, 1), (0, 1, 1), (1, 1, 1))
 
 
-def exchange_kernel(grad, opt_m, opt_v, master, m_new, v_new, w_new, gathered,
-                    acc, pair, half, quarter, eighth, m_buf, v_buf, w_buf, wb,
-                    load_sem, pair_send, pair_recv, half_send, half_recv, quarter_send, quarter_recv,
+def exchange_kernel(g_emb, g_attn, g_in, g_out, g_vec, opt_m, opt_v, master, m_new, v_new, w_new, gathered,
+                    stage, vec_buf, acc, pair, half, quarter, eighth, m_buf, v_buf, w_buf, wb,
+                    stage_sem, vec_sem, pair_send, pair_recv, half_send, half_recv, quarter_send, quarter_recv,
                     eighth_send, eighth_recv, state_sem, store_sem,
                     ring_send, ring_recv, share_send, share_recv, keep_sem):
     z, y, dx = lax.axis_index("dz"), lax.axis_index("dy"), lax.axis_index("dx")
@@ -162,80 +77,172 @@
     def rows(part):
         return pl.ds(PART_START[part], PART_ROWS[part])
 
-    barrier = pltpu.get_barrier_semaphore()
-    for peer in peers.values():
-        pl.semaphore_signal(barrier, inc=1, device_id=peer, device_id_type=MESH)
-    pl.semaphore_wait(barrier, 4)
-
+    def acc_rows(part):
+        return pl.ds(MARGIN + PART_START[part], PART_ROWS[part])
+
+    vec_load = pltpu.make_async_copy(g_vec, vec_buf, vec_sem)
     state = [
         pltpu.make_async_copy(opt_m, m_buf, state_sem.at[0]),
         pltpu.make_async_copy(opt_v, v_buf, state_sem.at[1]),
         pltpu.make_async_copy(master, w_buf, state_sem.at[2]),
     ]
 
-    units = [(b1,) + rest for b1 in (1, 0) for rest in HALF_ORDER]
     parts = (0, 1, 2)
 
-    def load(n, part):
-        where = chip(part, units[n])
-        return pltpu.make_async_copy(
-            grad.at[where, c, rows(part)], acc.at[where, rows(part)], load_sem.at[n, part])
+    def chip_at(n):
+        index = 0
+        for axis in "zyx":
+            index = index + WEIGHT[axis] * ((1 - mine[axis]) if axis in CHIP_ORDER[n] else mine[axis])
+        return index
+
+    def shard_at(n):
+        return 2 * chip_at(n % 8) + (1 - c if n < 8 else c)
+
+    def chunk_bounds(owner):
+        low = (owner * SHARD) // FLAT_ROWS
+        high = (owner * SHARD + SHARD + FLAT_ROWS - 1 - (owner // (DEVICES - 1)) * VEC_ROWS) // FLAT_ROWS
+        return low, high
+
+    def by_tensor(k, act):
+        @pl.when(k < 32)
+        def _():
+            act(0, 0)
+
+        @pl.when(k >= 32)
+        def _():
+            @pl.when(k < 80)
+            def _():
+                act(1, 32)
+
+            @pl.when(k >= 80)
+            def _():
+                @pl.when(k < 112)
+                def _():
+                    act(2, 80)
+
+                @pl.when(k >= 112)
+                def _():
+                    act(3, 112)
+
+    grads = (g_emb, g_attn, g_in, g_out)
+
+    def load_shard(n):
+        low, high = chunk_bounds(shard_at(n))
+        slot = n % STAGES
+
+        def one(k, carry):
+            where = k - low
+
+            def start(tensor, first):
+                pltpu.make_async_copy(
+                    grads[tensor].at[pl.ds((k - first) * TILES, TILES)], stage.at[slot, pl.ds(where * TILES, TILES)],
+                    stage_sem.at[slot, where]).start()
+
+            by_tensor(k, start)
+            return carry
+
+        lax.fori_loop(low, high, one, 0)
+
+    def flatten_shard(n):
+        owner = shard_at(n)
+        low, high = chunk_bounds(owner)
+        slot = n % STAGES
+        where = chip_at(n % 8)
+
+        def one(k, carry):
+            at = k - low
+            pltpu.make_async_copy(
+                g_emb.at[pl.ds(0, TILES)], stage.at[slot, pl.ds(at * TILES, TILES)], stage_sem.at[slot, at]).wait()
+            base = MARGIN + k * FLAT_ROWS - owner * SHARD
+
+            def spread(tensor, first):
+                groups = TENSORS[tensor][1] // LANES
+                bands = TILES // groups
+                for j in range(groups):
+                    tile = stage[slot, pl.ds(at * TILES + j, bands, stride=groups)]
+                    acc[where, pl.ds(base + j, 8 * bands, stride=groups), :] = tile.reshape(8 * bands, LANES)
+
+            by_tensor(k, spread)
+            return carry
+
+        lax.fori_loop(low, high, one, 0)
+
+        @pl.when(owner == DEVICES - 1)
+        def _():
+            first = MARGIN + SHARD - VEC_ROWS
+            acc[where, first:first + VEC_ROWS, :] = vec_buf[...]
 
     def pair_copy(n, part):
-        where = chip(part, units[n])
+        where = chip_at(n)
         return pltpu.make_async_remote_copy(
-            src_ref=grad.at[where, 1 - c, rows(part)], dst_ref=pair.at[where, rows(part)],
+            src_ref=acc.at[where, acc_rows(part)], dst_ref=pair.at[where, rows(part)],
             send_sem=pair_send.at[n, part], recv_sem=pair_recv.at[n, part],
             device_id=peers["c"], device_id_type=MESH)
 
     def half_copy(k, part):
         return pltpu.make_async_remote_copy(
-            src_ref=acc.at[chip(part, (1,) + HALF_ORDER[k]), rows(part)],
+            src_ref=acc.at[chip(part, (1,) + HALF_ORDER[k]), acc_rows(part)],
             dst_ref=half.at[part, k, pl.ds(0, PART_ROWS[part])],
             send_sem=half_send.at[k, part], recv_sem=half_recv.at[k, part],
             device_id=peers[ORDERS[part][0]], device_id_type=MESH)
 
     def quarter_copy(k, part):
         return pltpu.make_async_remote_copy(
-            src_ref=acc.at[chip(part, (0, 1, 1 - k)), rows(part)],
+            src_ref=acc.at[chip(part, (0, 1, 1 - k)), acc_rows(part)],
             dst_ref=quarter.at[part, k, pl.ds(0, PART_ROWS[part])],
             send_sem=quarter_send.at[k, part], recv_sem=quarter_recv.at[k, part],
             device_id=peers[ORDERS[part][1]], device_id_type=MESH)
 
     def eighth_copy(part):
         return pltpu.make_async_remote_copy(
-            src_ref=acc.at[chip(part, (0, 0, 1)), rows(part)],
+            src_ref=acc.at[chip(part, (0, 0, 1)), acc_rows(part)],
             dst_ref=eighth.at[part, pl.ds(0, PART_ROWS[part])],
             send_sem=eighth_send.at[part], recv_sem=eighth_recv.at[part],
             device_id=peers[ORDERS[part][2]], device_id_type=MESH)
 
+    vec_load.start()
+    for n in range(STAGES):
+        load_shard(n)
+    barrier = pltpu.get_barrier_semaphore()
+    for peer in peers.values():
+        pl.semaphore_signal(barrier, inc=1, device_id=peer, device_id_type=MESH)
+    pl.semaphore_wait(barrier, 4)
+    vec_load.wait()
+
+    for n in range(8):
+        flatten_shard(n)
+        for part in parts:
+            pair_copy(n, part).start()
+        if n + STAGES < 16:
+            load_shard(n + STAGES)
+    for copy in state:
+        copy.start()
+
     for n in range(8):
         for part in parts:
-            load(n, part).start()
-            pair_copy(n, part).start()
-    for copy in state:
-        copy.start()
-
-    for n in range(8):
+            pair_copy(n, part).wait_send()
+        flatten_shard(8 + n)
+        if 8 + n + STAGES < 16:
+            load_shard(8 + n + STAGES)
+        where = chip_at(n)
         for part in parts:
-            load(n, part).wait()
             pair_copy(n, part).wait_recv()
-            where = chip(part, units[n])
-            acc[where, rows(part)] += pair[where, rows(part)]
-            if n < 4:
-                half_copy(n, part).start()
+            acc[where, acc_rows(part)] += pair[where, rows(part)]
+            bits = tuple(int(axis in CHIP_ORDER[n]) for axis in ORDERS[part])
+            if bits[0]:
+                half_copy(HALF_ORDER.index(bits[1:]), part).start()
     for k in range(4):
         for part in parts:
             half_copy(k, part).wait_recv()
             where = chip(part, (0,) + HALF_ORDER[k])
-            acc[where, rows(part)] += half[part, k, pl.ds(0, PART_ROWS[part])]
+            acc[where, acc_rows(part)] += half[part, k, pl.ds(0, PART_ROWS[part])]
             if k < 2:
                 quarter_copy(k, part).start()
     for k in range(2):
         for part in parts:
             quarter_copy(k, part).wait_recv()
             where = chip(part, (0, 0, 1 - k))
-            acc[where, rows(part)] += quarter[part, k, pl.ds(0, PART_ROWS[part])]
+            acc[where, acc_rows(part)] += quarter[part, k, pl.ds(0, PART_ROWS[part])]
             if k == 0:
                 eighth_copy(part).start()
 
@@ -273,7 +280,7 @@
         pieces = [(start, count)] if count % 16 == 0 else [(start, count // 16 * 16), (start + count // 16 * 16, count % 16)]
         for first, size in pieces:
             span = pl.ds(first, size)
-            grad_sum = (acc[here, span] + eighth[part, pl.ds(first - start, size)]) / DEVICES
+            grad_sum = (acc[here, pl.ds(MARGIN + first, size)] + eighth[part, pl.ds(first - start, size)]) / DEVICES
             m_val = BETA_ONE * m_buf[span] + (1.0 - BETA_ONE) * grad_sum
             v_val = BETA_TWO * v_buf[span] + (1.0 - BETA_TWO) * grad_sum * grad_sum
             m_hat = m_val / (1.0 - BETA_ONE ** ADAM_STEP)
@@ -312,9 +319,6 @@
             share_copy(bits, part).start()
             keep_copy(bits, part).start()
 
-    for n in range(8):
-        for part in parts:
-            pair_copy(n, part).wait_send()
     for part in parts:
         for k in range(4):
             half_copy(k, part).wait_send()
@@ -330,29 +334,30 @@
         copy.wait()
 
 
-def exchange(grad, opt_m, opt_v, master):
+def exchange(*operands):
     shape = jax.ShapeDtypeStruct
     state_shape = shape((SHARD, LANES), jnp.float32)
     f32 = functools.partial(pltpu.VMEM, dtype=jnp.float32)
     dma = pltpu.SemaphoreType.DMA
     scratch = [
-        f32((8, PAD, LANES)), f32((8, PAD, LANES)),
+        f32((STAGES, SPAN * TILES, 8, LANES)), f32((VEC_ROWS, LANES)),
+        f32((8, SLOT, LANES)), f32((8, PAD, LANES)),
         f32((3, 4, PART_MAX, LANES)), f32((3, 2, PART_MAX, LANES)), f32((3, PART_MAX, LANES)),
         f32((SHARD, LANES)), f32((SHARD, LANES)), f32((SHARD, LANES)),
         pltpu.VMEM((8, PAD, LANES), jnp.bfloat16),
-        dma((8, 3)), dma((8, 3)), dma((8, 3)), dma((4, 3)), dma((4, 3)), dma((2, 3)), dma((2, 3)),
+        dma((STAGES, SPAN)), dma, dma((8, 3)), dma((8, 3)), dma((4, 3)), dma((4, 3)), dma((2, 3)), dma((2, 3)),
         dma((3,)), dma((3,)), dma((3,)), dma((3,)),
         dma((8, 3)), dma((8, 3)), dma((8, 3)), dma((8, 3)), dma((8, 3)),
     ]
     return pl.pallas_call(
         exchange_kernel,
         out_shape=(state_shape, state_shape, state_shape, shape((8, 2, PAD, LANES), jnp.bfloat16)),
-        in_specs=[pl.BlockSpec(memory_space=pl.ANY)] * 4,
+        in_specs=[pl.BlockSpec(memory_space=pl.ANY)] * 8,
         out_specs=(pl.BlockSpec(memory_space=pl.ANY),) * 4,
         scratch_shapes=scratch,
         compiler_params=pltpu.CompilerParams(vmem_limit_bytes=VMEM_MAX, collective_id=0, has_side_effects=True),
         name="exchange",
-    )(grad, opt_m, opt_v, master)
+    )(*operands)
 
 
 SUB = 512
@@ -574,9 +579,12 @@
         vec = jnp.concatenate([
             g_vecd.reshape(-1, LANES), g_vecf.reshape(-1, LANES),
             jnp.zeros((VEC_ROWS - (9 * D + FF) // LANES, LANES), jnp.float32)], axis=0)
-        grad = flatten(g_emb.reshape(VOCAB, D), g_attn.reshape(4 * D, D), g_in.reshape(D, FF), g_out.reshape(FF, D), vec)
+        def tiles(grad, cols):
+            split = grad.reshape(-1, 8, cols // LANES, LANES)
+            return split.transpose(0, 2, 1, 3).reshape(-1, 8, LANES)
+
         m_new, v_new, w_new, gathered = exchange(
-            grad.reshape(8, 2, PAD, LANES), opt_m.reshape(SHARD, LANES),
+            tiles(g_emb, D), tiles(g_attn, D), tiles(g_in, FF), tiles(g_out, D), vec, opt_m.reshape(SHARD, LANES),
             opt_v.reshape(SHARD, LANES), master.reshape(SHARD, LANES))
         flat = gathered.reshape(DEVICES, PAD, LANES)
         y_out, wb_emb, wb_attn, wb_in, wb_out, wb_vecd, wb_vecf, m_new, v_new, w_new = ffn(

time: 317 us -> 299 us (0.943)
  Pallas kernels: 313 us -> 295 us
    pallas_call x1 -> x0, Pallas kernels: 19.6 us -> none  [flatten(): pl.pallas_call(flatten_kernel, out_shape=jax.ShapeDtypeStruct((DEVICES, P...]
where the time goes in v3:
time: 299 us
  Pallas kernels  295 us (99%)
    pallas_call x1, Pallas kernels, exchange(): pl.pallas_call(exchange_kernel, out_shape=(state_shape, state_shape, stat...  152 us
    pallas_call x1, Pallas kernels, ffn(): pl.pallas_call(functools.partial(ffn_kernel, steps), out_shape=(shape((to...  144 us

profile of v3, /device:TPU:0, one launch (start us, length us, event | category | flops | bytes accessed | tf_op | source)
XLA Modules:
  0.0 298.5 jit_solution(15836514391246404250)
XLA Ops:
  0.7 0.1 pad.2.clone
  0.7 0.8 reduce
  1.6 1.4 maximum_maximum_fusion.g_vec
  3.0 151.6 %exchange.1 = (f32[3461,128]{1,0:T(8,128)}, f32[3461,128]{1,0:T(8,128)}, f32[3461,128]{1,0:T(8,128)}, bf16[8,2,3472,128]{3,2,1,0:T(8,128)(2,1)}) custom-call(f32[1536,8,128]{2,1,0:T(8,128)} %bitcast.34, f32[2304,8,128]{2,1,0:T(8,128)} %bitcast.33, f32[1536,8,128]{2,1,0:T(8,128)} %bitcast.35, f32[1536,8,128]{2,1,0:T(8,128)} %bitcast.36, ...), custom_call_target="tpu_custom_call" | custom-call | tf_op jit(solution)/shard_map/exchange/pallas_call | solution.py:352
  154.6 143.8 %ffn.1 = (bf16[16384,768]{1,0:T(8,128)(2,1)}, bf16[2048,768]{1,0:T(8,128)(2,1)}, bf16[3072,768]{1,0:T(8,128)(2,1)}, bf16[768,2048]{1,0:T(8,128)(2,1)}, bf16[2048...) custom-call(s32[16384]{0:T(1024)} %ids.1, ...), custom_call_target="tpu_custom_call" | custom-call | tf_op jit(solution)/shard_map/ffn/pallas_call | solution.py:543
  (2 shorter events, 0.0 us)

commit v4 on v3

--- a/solution.py
+++ b/solution.py
@@ -24,9 +24,10 @@
 LANES = 128
 SHARD = 3461
 PAD = 3472
-PART_START = (0, 1152, 2304)
-PART_ROWS = (1152, 1152, 1168)
-PART_MAX = 1168
+PART_START = (0, 576, 1152, 1728, 2304, 2880)
+PART_ROWS = (576, 576, 576, 576, 576, 592)
+PART_MAX = 592
+PARTS = 6
 VMEM_MAX = 67_000_000
 
 TENSORS = (
@@ -46,15 +47,15 @@
 VEC_ROWS = DEVICES * SHARD - VEC_BASE
 
 
-ORDERS = (("x", "y", "z"), ("y", "z", "x"), ("z", "x", "y"))
+ORDERS = (("x", "y", "z"), ("y", "z", "x"), ("z", "x", "y")) * 2
 WEIGHT = {"z": 4, "y": 2, "x": 1}
 CHIP_ORDER = ("xyz", "xy", "yz", "zx", "x", "y", "z", "")
 HALF_ORDER = ((1, 1), (1, 0), (0, 1), (0, 0))
 GATHER_ORDER = ((1, 0, 0), (0, 1, 0), (0, 0, 1), (1, 1, 0), (1, 0, 1), (0, 1, 1), (1, 1, 1))
 
 
-def exchange_kernel(g_emb, g_attn, g_in, g_out, g_vec, opt_m, opt_v, master, m_new, v_new, w_new, gathered,
-                    stage, vec_buf, acc, pair, half, quarter, eighth, m_buf, v_buf, w_buf, wb,
+def exchange_kernel(g_emb, g_attn, g_in, g_out, g_vecd, g_vecf, opt_m, opt_v, master, m_new, v_new, w_new, gathered,
+                    stage, vecd_buf, vecf_buf, acc, pair, half, quarter, eighth, m_buf, v_buf, w_buf, wb,
                     stage_sem, vec_sem, pair_send, pair_recv, half_send, half_recv, quarter_send, quarter_recv,
                     eighth_send, eighth_recv, state_sem, store_sem,
                     ring_send, ring_recv, share_send, share_recv, keep_sem):
@@ -80,14 +81,15 @@
     def acc_rows(part):
         return pl.ds(MARGIN + PART_START[part], PART_ROWS[part])
 
-    vec_load = pltpu.make_async_copy(g_vec, vec_buf, vec_sem)
+    vec_loads = [
+        pltpu.make_async_copy(g_vecd, vecd_buf, vec_sem.at[0]), pltpu.make_async_copy(g_vecf, vecf_buf, vec_sem.at[1])]
     state = [
         pltpu.make_async_copy(opt_m, m_buf, state_sem.at[0]),
         pltpu.make_async_copy(opt_v, v_buf, state_sem.at[1]),
         pltpu.make_async_copy(master, w_buf, state_sem.at[2]),
     ]
 
-    parts = (0, 1, 2)
+    parts = range(PARTS)
 
     def chip_at(n):
         index = 0
@@ -95,8 +97,14 @@
             index = index + WEIGHT[axis] * ((1 - mine[axis]) if axis in CHIP_ORDER[n] else mine[axis])
         return index
 
-    def shard_at(n):
-        return 2 * chip_at(n % 8) + (1 - c if n < 8 else c)
+    sequence = [(False, 0)]
+    for n in range(1, 8):
+        sequence += [(False, n), (True, n - 1)]
+    sequence.append((True, 7))
+
+    def shard_at(place):
+        own, n = sequence[place]
+        return 2 * chip_at(n) + (c if own else 1 - c)
 
     def chunk_bounds(owner):
         low = (owner * SHARD) // FLAT_ROWS
@@ -126,9 +134,9 @@
 
     grads = (g_emb, g_attn, g_in, g_out)
 
-    def load_shard(n):
-        low, high = chunk_bounds(shard_at(n))
-        slot = n % STAGES
+    def load_shard(place):
+        low, high = chunk_bounds(shard_at(place))
+        slot = place % STAGES
 
         def one(k, carry):
             where = k - low
@@ -143,11 +151,11 @@
 
         lax.fori_loop(low, high, one, 0)
 
-    def flatten_shard(n):
-        owner = shard_at(n)
+    def flatten_shard(place):
+        owner = shard_at(place)
         low, high = chunk_bounds(owner)
-        slot = n % STAGES
-        where = chip_at(n % 8)
+        slot = place % STAGES
+        where = chip_at(sequence[place][1])
 
         def one(k, carry):
             at = k - low
@@ -170,7 +178,11 @@
         @pl.when(owner == DEVICES - 1)
         def _():
             first = MARGIN + SHARD - VEC_ROWS
-            acc[where, first:first + VEC_ROWS, :] = vec_buf[...]
+            second = first + 9 * D // LANES
+            third = second + FF // LANES
+            acc[where, first:second, :] = vecd_buf[...]
+            acc[where, second:third, :] = vecf_buf[...]
+            acc[where, third:MARGIN + SHARD, :] = jnp.zeros((MARGIN + SHARD - third, LANES), jnp.float32)
 
     def pair_copy(n, part):
         where = chip_at(n)
@@ -200,37 +212,36 @@
             send_sem=eighth_send.at[part], recv_sem=eighth_recv.at[part],
             device_id=peers[ORDERS[part][2]], device_id_type=MESH)
 
-    vec_load.start()
-    for n in range(STAGES):
-        load_shard(n)
+    for place in range(STAGES):
+        load_shard(place)
+    for copy in vec_loads:
+        copy.start()
     barrier = pltpu.get_barrier_semaphore()
     for peer in peers.values():
         pl.semaphore_signal(barrier, inc=1, device_id=peer, device_id_type=MESH)
     pl.semaphore_wait(barrier, 4)
-    vec_load.wait()
-
-    for n in range(8):
-        flatten_shard(n)
-        for part in parts:
-            pair_copy(n, part).start()
-        if n + STAGES < 16:
-            load_shard(n + STAGES)
-    for copy in state:
-        copy.start()
-
-    for n in range(8):
-        for part in parts:
-            pair_copy(n, part).wait_send()
-        flatten_shard(8 + n)
-        if 8 + n + STAGES < 16:
-            load_shard(8 + n + STAGES)
+    for copy in vec_loads:
+        copy.wait()
+
+    for place, (own, n) in enumerate(sequence):
+        if own:
+            for part in parts:
+                pair_copy(n, part).wait_send()
+        flatten_shard(place)
+        if place + STAGES < len(sequence):
+            load_shard(place + STAGES)
         where = chip_at(n)
         for part in parts:
+            if not own:
+                pair_copy(n, part).start()
+                continue
             pair_copy(n, part).wait_recv()
             acc[where, acc_rows(part)] += pair[where, rows(part)]
             bits = tuple(int(axis in CHIP_ORDER[n]) for axis in ORDERS[part])
             if bits[0]:
                 half_copy(HALF_ORDER.index(bits[1:]), part).start()
+    for copy in state:
+        copy.start()
     for k in range(4):
         for part in parts:
             half_copy(k, part).wait_recv()
@@ -340,19 +351,20 @@
     f32 = functools.partial(pltpu.VMEM, dtype=jnp.float32)
     dma = pltpu.SemaphoreType.DMA
     scratch = [
-        f32((STAGES, SPAN * TILES, 8, LANES)), f32((VEC_ROWS, LANES)),
+        f32((STAGES, SPAN * TILES, 8, LANES)), f32((9 * D // LANES, LANES)), f32((FF // LANES, LANES)),
         f32((8, SLOT, LANES)), f32((8, PAD, LANES)),
-        f32((3, 4, PART_MAX, LANES)), f32((3, 2, PART_MAX, LANES)), f32((3, PART_MAX, LANES)),
+        f32((PARTS, 4, PART_MAX, LANES)), f32((PARTS, 2, PART_MAX, LANES)), f32((PARTS, PART_MAX, LANES)),
         f32((SHARD, LANES)), f32((SHARD, LANES)), f32((SHARD, LANES)),
         pltpu.VMEM((8, PAD, LANES), jnp.bfloat16),
-        dma((STAGES, SPAN)), dma, dma((8, 3)), dma((8, 3)), dma((4, 3)), dma((4, 3)), dma((2, 3)), dma((2, 3)),
-        dma((3,)), dma((3,)), dma((3,)), dma((3,)),
-        dma((8, 3)), dma((8, 3)), dma((8, 3)), dma((8, 3)), dma((8, 3)),
+        dma((STAGES, SPAN)), dma((2,)), dma((8, PARTS)), dma((8, PARTS)),
+        dma((4, PARTS)), dma((4, PARTS)), dma((2, PARTS)), dma((2, PARTS)),
+        dma((PARTS,)), dma((PARTS,)), dma((3,)), dma((3,)),
+        dma((8, PARTS)), dma((8, PARTS)), dma((8, PARTS)), dma((8, PARTS)), dma((8, PARTS)),
     ]
     return pl.pallas_call(
         exchange_kernel,
         out_shape=(state_shape, state_shape, state_shape, shape((8, 2, PAD, LANES), jnp.bfloat16)),
-        in_specs=[pl.BlockSpec(memory_space=pl.ANY)] * 8,
+        in_specs=[pl.BlockSpec(memory_space=pl.ANY)] * 9,
         out_specs=(pl.BlockSpec(memory_space=pl.ANY),) * 4,
         scratch_shapes=scratch,
         compiler_params=pltpu.CompilerParams(vmem_limit_bytes=VMEM_MAX, collective_id=0, has_side_effects=True),
@@ -361,9 +373,10 @@
 
 
 SUB = 512
-CHUNK = 2 * SUB
+UNROLL = 2
+CHUNK = UNROLL * SUB
 RING = 6
-ACT_SLOTS = 3
+ACT_SLOTS = 2 * UNROLL
 GELU_A = math.sqrt(2.0 / math.pi)
 GELU_B = GELU_A * 0.044715
 WIDEN_ORDER = (8, 9, 10, 11, 12, 13, 14, 15, 0, 1, 2, 3, 4, 5, 6, 7)
@@ -376,9 +389,11 @@
                ring_sem, act_sem, y_sem, emb_sem, attn_sem, weight_sem, state_sem):
     emb_rows, attn_rows = VOCAB // steps, 4 * D // steps
 
-    def load_act(it):
-        return pltpu.make_async_copy(
-            act.at[pl.ds(it * CHUNK, CHUNK)], act_buf.at[lax.rem(it, ACT_SLOTS)], act_sem.at[lax.rem(it, ACT_SLOTS)])
+    blocks = steps * UNROLL
+
+    def load_act(block):
+        slot = lax.rem(block, ACT_SLOTS)
+        return pltpu.make_async_copy(act.at[pl.ds(block * SUB, SUB)], act_buf.at[slot], act_sem.at[slot])
 
     def store_y(it):
         return pltpu.make_async_copy(
@@ -397,8 +412,8 @@
 
     for n in range(RING):
         load_flat(n).start()
-    load_act(0).start()
-    load_act(1).start()
+    for block in range(UNROLL + 1):
+        load_act(block).start()
 
     def relayout(base, groups, row, buf, at):
         for j in range(groups):
@@ -453,9 +468,9 @@
             pltpu.make_async_copy(vecd_buf, o_vecd, weight_sem.at[2]).start()
             pltpu.make_async_copy(vecf_buf, o_vecf, weight_sem.at[3]).start()
 
-    def lookup(it, half, h_buf, rows_buf):
-        slot = lax.rem(it, ACT_SLOTS)
-        token = jnp.minimum(it, steps - 1) * CHUNK + half * SUB
+    def lookup(block, h_buf, rows_buf):
+        slot = lax.rem(block, ACT_SLOTS)
+        token = jnp.minimum(block, blocks - 1) * SUB
         for tile in range(SUB // 8):
             for i in range(8):
                 row = ids[token + tile * 8 + i] * (D // LANES)
@@ -465,20 +480,19 @@
                 top = rows_buf[pl.ds(pair * 112 + j, 8, stride=7), :]
                 low = rows_buf[pl.ds(pair * 112 + 56 + j, 8, stride=7), :]
                 both = jnp.concatenate([top, low], axis=0) * math.sqrt(D)
-                first = half * SUB + pair * 16
-                a_val = act_buf[slot, first:first + 16, j * LANES:(j + 1) * LANES].astype(jnp.float32)
+                a_val = act_buf[slot, pair * 16:pair * 16 + 16, j * LANES:(j + 1) * LANES].astype(jnp.float32)
                 h_buf[pair * 16:pair * 16 + 16, j * LANES:(j + 1) * LANES] = (both + a_val).astype(jnp.bfloat16)
 
-    def multiply(it, half, h_buf, u_buf):
+    def multiply(it, part, h_buf, u_buf):
         pre = jnp.dot(h_buf[...], w_in[...], preferred_element_type=jnp.float32) + b_in[...]
         bent = jnp.tanh(pre * (GELU_A + GELU_B * (pre * pre)))
-        part = 0.5 * pre
-        u_buf[...] = (part + part * bent).astype(jnp.bfloat16)
+        flat_half = 0.5 * pre
+        u_buf[...] = (flat_half + flat_half * bent).astype(jnp.bfloat16)
         y_val = jnp.dot(u_buf[...], w_out[...], preferred_element_type=jnp.float32) + b_out[...]
-        y_buf[lax.rem(it, 2), half * SUB:half * SUB + SUB, :] = y_val.astype(jnp.bfloat16)
+        y_buf[lax.rem(it, 2), part * SUB:part * SUB + SUB, :] = y_val.astype(jnp.bfloat16)
 
     load_act(0).wait()
-    lookup(0, 0, h_one, rows_one)
+    lookup(0, h_one, rows_one)
 
     moves = []
     for n, (source, target) in enumerate(((m_in, m_out), (v_in, v_out), (master_in, master_out))):
@@ -486,13 +500,18 @@
         moves.append(pltpu.make_async_copy(state_buf, target, state_sem.at[2 * n + 1]))
 
     def body(it, carry):
+        for part in range(1, UNROLL):
+            load_act(it * UNROLL + part).wait()
+
         @pl.when(it + 1 < steps)
         def _():
-            load_act(it + 1).wait()
+            load_act(it * UNROLL + UNROLL).wait()
+            for part in range(UNROLL + 1, 2 * UNROLL):
+                load_act(it * UNROLL + part).start()
 
         @pl.when(it + 2 < steps)
         def _():
-            load_act(it + 2).start()
+            load_act(it * UNROLL + 2 * UNROLL).start()
 
         @pl.when(it >= 2)
         def _():
@@ -501,16 +520,18 @@
             store_attn(it - 2).wait()
 
         for n, move in enumerate(moves):
-            @pl.when(it == 1 + 2 * n)
+            @pl.when(it == 1 + n)
             def _(n=n, move=move):
                 if n:
                     moves[n - 1].wait()
                 move.start()
 
-        lookup(it, 1, h_two, rows_two)
-        multiply(it, 0, h_one, u_one)
-        lookup(it + 1, 0, h_one, rows_one)
-        multiply(it, 1, h_two, u_two)
+        buffers = ((h_one, rows_one, u_one), (h_two, rows_two, u_two))
+        for part in range(UNROLL):
+            h_now, _, u_now = buffers[part % 2]
+            h_next, rows_next, _ = buffers[(part + 1) % 2]
+            lookup(it * UNROLL + part + 1, h_next, rows_next)
+            multiply(it, part, h_now, u_now)
         for t in range(emb_rows // 16):
             relayout(TENSORS[0][2], D // LANES, it * emb_rows + t * 16, emb_buf.at[lax.rem(it, 2)], t * 16)
         for t in range(attn_rows // 16):
@@ -549,7 +570,7 @@
         scratch_shapes=[
             pltpu.VMEM((DEVICES * SHARD, LANES), f32),
             pltpu.VMEM((RING, PAD, LANES), bf16),
-            pltpu.VMEM((ACT_SLOTS, CHUNK, D), bf16),
+            pltpu.VMEM((ACT_SLOTS, SUB, D), bf16),
             pltpu.VMEM((2, CHUNK, D), bf16),
             pltpu.VMEM((D, FF), bf16),
             pltpu.VMEM((FF, D), bf16),
@@ -576,15 +597,13 @@
 
 def solution(mesh):
     def device_step(g_emb, g_attn, g_in, g_out, g_vecd, g_vecf, opt_m, opt_v, master, tok_ids, act_in):
-        vec = jnp.concatenate([
-            g_vecd.reshape(-1, LANES), g_vecf.reshape(-1, LANES),
-            jnp.zeros((VEC_ROWS - (9 * D + FF) // LANES, LANES), jnp.float32)], axis=0)
         def tiles(grad, cols):
             split = grad.reshape(-1, 8, cols // LANES, LANES)
             return split.transpose(0, 2, 1, 3).reshape(-1, 8, LANES)
 
         m_new, v_new, w_new, gathered = exchange(
-            tiles(g_emb, D), tiles(g_attn, D), tiles(g_in, FF), tiles(g_out, D), vec, opt_m.reshape(SHARD, LANES),
+            tiles(g_emb, D), tiles(g_attn, D), tiles(g_in, FF), tiles(g_out, D),
+            g_vecd.reshape(-1, LANES), g_vecf.reshape(-1, LANES), opt_m.reshape(SHARD, LANES),
             opt_v.reshape(SHARD, LANES), master.reshape(SHARD, LANES))
         flat = gathered.reshape(DEVICES, PAD, LANES)
         y_out, wb_emb, wb_attn, wb_in, wb_out, wb_vecd, wb_vecf, m_new, v_new, w_new = ffn(

time: 299 us -> 298 us (level)
  no operation moved by 1% of the time
where the time goes in v4:
time: 298 us; the launch traced here: 297 us
  Pallas kernels  295 us (99%)
    pallas_call x1, Pallas kernels, exchange(): pl.pallas_call(exchange_kernel, out_shape=(state_shape, state_shape, stat...  151 us
    pallas_call x1, Pallas kernels, ffn(): pl.pallas_call(functools.partial(ffn_kernel, steps), out_shape=(shape((to...  144 us

profile of v4, /device:TPU:0, one launch (start us, length us, event | category | flops | bytes accessed | tf_op | source)
XLA Modules:
  0.0 297.3 jit_solution(13281954650859518989)
XLA Ops:
  0.6 0.8 reduce
  1.5 0.6 reshape.82.g_vecd
  2.1 151.4 %exchange.1 = (f32[3461,128]{1,0:T(8,128)}, f32[3461,128]{1,0:T(8,128)}, f32[3461,128]{1,0:T(8,128)}, bf16[8,2,3472,128]{3,2,1,0:T(8,128)(2,1)}) custom-call(f32[1536,8,128]{2,1,0:T(8,128)} %bitcast.34, f32[2304,8,128]{2,1,0:T(8,128)} %bitcast.33, f32[1536,8,128]{2,1,0:T(8,128)} %bitcast.35, f32[1536,8,128]{2,1,0:T(8,128)} %bitcast.36, ...), custom_call_target="tpu_custom_call" | custom-call | tf_op jit(solution)/shard_map/exchange/pallas_call | solution.py:364
  153.5 143.6 %ffn.1 = (bf16[16384,768]{1,0:T(8,128)(2,1)}, bf16[2048,768]{1,0:T(8,128)(2,1)}, bf16[3072,768]{1,0:T(8,128)(2,1)}, bf16[768,2048]{1,0:T(8,128)(2,1)}, bf16[2048...) custom-call(s32[16384]{0:T(1024)} %ids.1, ...), custom_call_target="tpu_custom_call" | custom-call | tf_op jit(solution)/shard_map/ffn/pallas_call | solution.py:564

commit v5 on v4

--- a/solution.py
+++ b/solution.py
@@ -397,7 +397,12 @@
 
     def store_y(it):
         return pltpu.make_async_copy(
-            y_buf.at[lax.rem(it, 2)], y_out.at[pl.ds(it * CHUNK, CHUNK)], y_sem.at[lax.rem(it, 2)])
+            y_buf.at[lax.rem(it, 2)], y_out.at[pl.ds(it * CHUNK - SUB, CHUNK)], y_sem.at[lax.rem(it, 2)])
+
+    store_first = pltpu.make_async_copy(
+        y_buf.at[0, pl.ds(SUB, CHUNK - SUB)], y_out.at[pl.ds(0, CHUNK - SUB)], y_sem.at[0])
+    store_last = pltpu.make_async_copy(
+        y_buf.at[steps % 2, pl.ds(0, SUB)], y_out.at[pl.ds(steps * CHUNK - SUB, SUB)], y_sem.at[steps % 2])
 
     def store_emb(it):
         return pltpu.make_async_copy(
@@ -483,11 +488,13 @@
                 a_val = act_buf[slot, pair * 16:pair * 16 + 16, j * LANES:(j + 1) * LANES].astype(jnp.float32)
                 h_buf[pair * 16:pair * 16 + 16, j * LANES:(j + 1) * LANES] = (both + a_val).astype(jnp.bfloat16)
 
-    def multiply(it, part, h_buf, u_buf):
+    def widen_tokens(h_buf, u_buf):
         pre = jnp.dot(h_buf[...], w_in[...], preferred_element_type=jnp.float32) + b_in[...]
         bent = jnp.tanh(pre * (GELU_A + GELU_B * (pre * pre)))
         flat_half = 0.5 * pre
         u_buf[...] = (flat_half + flat_half * bent).astype(jnp.bfloat16)
+
+    def narrow_tokens(it, part, u_buf):
         y_val = jnp.dot(u_buf[...], w_out[...], preferred_element_type=jnp.float32) + b_out[...]
         y_buf[lax.rem(it, 2), part * SUB:part * SUB + SUB, :] = y_val.astype(jnp.bfloat16)
 
@@ -513,9 +520,16 @@
         def _():
             load_act(it * UNROLL + 2 * UNROLL).start()
 
+        @pl.when(it == 2)
+        def _():
+            store_first.wait()
+
+        @pl.when(it > 2)
+        def _():
+            store_y(it - 2).wait()
+
         @pl.when(it >= 2)
         def _():
-            store_y(it - 2).wait()
             store_emb(it - 2).wait()
             store_attn(it - 2).wait()
 
@@ -529,21 +543,33 @@
         buffers = ((h_one, rows_one, u_one), (h_two, rows_two, u_two))
         for part in range(UNROLL):
             h_now, _, u_now = buffers[part % 2]
-            h_next, rows_next, _ = buffers[(part + 1) % 2]
+            h_next, rows_next, u_before = buffers[(part + 1) % 2]
             lookup(it * UNROLL + part + 1, h_next, rows_next)
-            multiply(it, part, h_now, u_now)
+            widen_tokens(h_now, u_now)
+            narrow_tokens(it, part, u_before)
         for t in range(emb_rows // 16):
             relayout(TENSORS[0][2], D // LANES, it * emb_rows + t * 16, emb_buf.at[lax.rem(it, 2)], t * 16)
         for t in range(attn_rows // 16):
             relayout(TENSORS[1][2], D // LANES, it * attn_rows + t * 16, attn_buf.at[lax.rem(it, 2)], t * 16)
-        store_y(it).start()
+        @pl.when(it == 0)
+        def _():
+            store_first.start()
+
+        @pl.when(it > 0)
+        def _():
+            store_y(it).start()
+
         store_emb(it).start()
         store_attn(it).start()
         return carry
 
     lax.fori_loop(0, steps, body, 0)
+    store_y(steps - 2).wait()
+    narrow_tokens(steps, 0, u_two)
+    store_last.start()
+    store_y(steps - 1).wait()
+    store_last.wait()
     for it in (steps - 2, steps - 1):
-        store_y(it).wait()
         store_emb(it).wait()
         store_attn(it).wait()
     moves[-1].wait()

time: 298 us -> 298 us (level)
  no operation moved by 1% of the time
where the time goes in v5:
time: 298 us
  Pallas kernels  295 us (99%)
    pallas_call x1, Pallas kernels, exchange(): pl.pallas_call(exchange_kernel, out_shape=(state_shape, state_shape, stat...  151 us
    pallas_call x1, Pallas kernels, ffn(): pl.pallas_call(functools.partial(ffn_kernel, steps), out_shape=(shape((to...  144 us

profile of v5, /device:TPU:0, one launch (start us, length us, event | category | flops | bytes accessed | tf_op | source)
XLA Modules:
  0.0 297.6 jit_solution(17556354229042038328)
XLA Ops:
  0.6 0.8 reduce
  1.5 0.6 reshape.82.g_vecd
  2.1 151.4 %exchange.1 = (f32[3461,128]{1,0:T(8,128)}, f32[3461,128]{1,0:T(8,128)}, f32[3461,128]{1,0:T(8,128)}, bf16[8,2,3472,128]{3,2,1,0:T(8,128)(2,1)}) custom-call(f32[1536,8,128]{2,1,0:T(8,128)} %bitcast.34, f32[2304,8,128]{2,1,0:T(8,128)} %bitcast.33, f32[1536,8,128]{2,1,0:T(8,128)} %bitcast.35, f32[1536,8,128]{2,1,0:T(8,128)} %bitcast.36, ...), custom_call_target="tpu_custom_call" | custom-call | tf_op jit(solution)/shard_map/exchange/pallas_call | solution.py:364
  153.5 143.9 %ffn.1 = (bf16[16384,768]{1,0:T(8,128)(2,1)}, bf16[2048,768]{1,0:T(8,128)(2,1)}, bf16[3072,768]{1,0:T(8,128)(2,1)}, bf16[768,2048]{1,0:T(8,128)(2,1)}, bf16[2048...) custom-call(s32[16384]{0:T(1024)} %ids.1, ...), custom_call_target="tpu_custom_call" | custom-call | tf_op jit(solution)/shard_map/ffn/pallas_call | solution.py:590

commit v6 on v5

--- a/solution.py
+++ b/solution.py
@@ -55,7 +55,7 @@
 
 
 def exchange_kernel(g_emb, g_attn, g_in, g_out, g_vecd, g_vecf, opt_m, opt_v, master, m_new, v_new, w_new, gathered,
-                    stage, vecd_buf, vecf_buf, acc, pair, half, quarter, eighth, m_buf, v_buf, w_buf, wb,
+                    stage, vecd_raw, vecd_buf, vecf_buf, acc, pair, half, quarter, eighth, m_buf, v_buf, w_buf, wb,
                     stage_sem, vec_sem, pair_send, pair_recv, half_send, half_recv, quarter_send, quarter_recv,
                     eighth_send, eighth_recv, state_sem, store_sem,
                     ring_send, ring_recv, share_send, share_recv, keep_sem):
@@ -82,7 +82,7 @@
         return pl.ds(MARGIN + PART_START[part], PART_ROWS[part])
 
     vec_loads = [
-        pltpu.make_async_copy(g_vecd, vecd_buf, vec_sem.at[0]), pltpu.make_async_copy(g_vecf, vecf_buf, vec_sem.at[1])]
+        pltpu.make_async_copy(g_vecd, vecd_raw, vec_sem.at[0]), pltpu.make_async_copy(g_vecf, vecf_buf, vec_sem.at[1])]
     state = [
         pltpu.make_async_copy(opt_m, m_buf, state_sem.at[0]),
         pltpu.make_async_copy(opt_v, v_buf, state_sem.at[1]),
@@ -222,6 +222,10 @@
     pl.semaphore_wait(barrier, 4)
     for copy in vec_loads:
         copy.wait()
+    for i in range(9):
+        for j in range(D // LANES):
+            row = i * (D // LANES) + j
+            vecd_buf[row:row + 1, :] = vecd_raw[i, :, j * LANES:(j + 1) * LANES]
 
     for place, (own, n) in enumerate(sequence):
         if own:
@@ -351,7 +355,8 @@
     f32 = functools.partial(pltpu.VMEM, dtype=jnp.float32)
     dma = pltpu.SemaphoreType.DMA
     scratch = [
-        f32((STAGES, SPAN * TILES, 8, LANES)), f32((9 * D // LANES, LANES)), f32((FF // LANES, LANES)),
+        f32((STAGES, SPAN * TILES, 8, LANES)), f32((9, 1, D)), f32((9 * D // LANES, LANES)),
+        f32((FF // LANES, LANES)),
         f32((8, SLOT, LANES)), f32((8, PAD, LANES)),
         f32((PARTS, 4, PART_MAX, LANES)), f32((PARTS, 2, PART_MAX, LANES)), f32((PARTS, PART_MAX, LANES)),
         f32((SHARD, LANES)), f32((SHARD, LANES)), f32((SHARD, LANES)),
@@ -382,11 +387,11 @@
 WIDEN_ORDER = (8, 9, 10, 11, 12, 13, 14, 15, 0, 1, 2, 3, 4, 5, 6, 7)
 
 
-def ffn_kernel(steps, ids, act, flat, m_in, v_in, master_in,
+def ffn_kernel(steps, ids_in, act, flat, m_in, v_in, master_in,
                y_out, o_emb, o_attn, o_in, o_out, o_vecd, o_vecf, m_out, v_out, master_out,
-               dense, ring, act_buf, y_buf, w_in, w_out, b_in, b_out, vecd_wide, vecd_buf, vecf_buf,
+               ids, dense, ring, act_buf, y_buf, w_in, w_out, b_in, b_out, vecd_wide, vecd_buf, vecf_buf,
                rows_one, rows_two, h_one, h_two, u_one, u_two, emb_buf, attn_buf, state_buf,
-               ring_sem, act_sem, y_sem, emb_sem, attn_sem, weight_sem, state_sem):
+               ring_sem, act_sem, y_sem, emb_sem, attn_sem, weight_sem, state_sem, ids_sem):
     emb_rows, attn_rows = VOCAB // steps, 4 * D // steps
 
     blocks = steps * UNROLL
@@ -417,6 +422,8 @@
 
     for n in range(RING):
         load_flat(n).start()
+    load_ids = pltpu.make_async_copy(ids_in, ids, ids_sem)
+    load_ids.start()
     for block in range(UNROLL + 1):
         load_act(block).start()
 
@@ -448,7 +455,7 @@
                 relayout(TENSORS[2][2], FF // LANES, row, w_in, row)
                 return carry
 
-            lax.fori_loop(0, D // 16, fill_in, 0, unroll=2)
+            lax.fori_loop(0, D // 16, fill_in, 0, unroll=4)
             pltpu.make_async_copy(w_in, o_in, weight_sem.at[0]).start()
         if owner == 15:
             def fill_out(t, carry):
@@ -456,7 +463,7 @@
                 relayout(TENSORS[3][2], D // LANES, row, w_out, row)
                 return carry
 
-            lax.fori_loop(0, FF // 16, fill_out, 0, unroll=4)
+            lax.fori_loop(0, FF // 16, fill_out, 0, unroll=8)
             pltpu.make_async_copy(w_out, o_out, weight_sem.at[1]).start()
             for i in range(9):
                 for j in range(D // LANES):
@@ -498,6 +505,7 @@
         y_val = jnp.dot(u_buf[...], w_out[...], preferred_element_type=jnp.float32) + b_out[...]
         y_buf[lax.rem(it, 2), part * SUB:part * SUB + SUB, :] = y_val.astype(jnp.bfloat16)
 
+    load_ids.wait()
     load_act(0).wait()
     lookup(0, h_one, rows_one)
 
@@ -591,9 +599,10 @@
         functools.partial(ffn_kernel, steps),
         out_shape=(shape((tokens, D), bf16), shape((VOCAB, D), bf16), shape((4 * D, D), bf16), shape((D, FF), bf16),
                    shape((FF, D), bf16), shape((9, D), bf16), shape((1, FF), bf16), state, state, state),
-        in_specs=[pl.BlockSpec(memory_space=pltpu.SMEM)] + [anywhere] * 5,
+        in_specs=[anywhere] * 6,
         out_specs=(anywhere,) * 10,
         scratch_shapes=[
+            pltpu.SMEM((tokens,), jnp.int32),
             pltpu.VMEM((DEVICES * SHARD, LANES), f32),
             pltpu.VMEM((RING, PAD, LANES), bf16),
             pltpu.VMEM((ACT_SLOTS, SUB, D), bf16),
@@ -614,7 +623,7 @@
             pltpu.VMEM((2, VOCAB // steps, D), bf16),
             pltpu.VMEM((2, 4 * D // steps, D), bf16),
             pltpu.VMEM((SHARD, LANES), f32),
-            dma((RING,)), dma((ACT_SLOTS,)), dma((2,)), dma((2,)), dma((2,)), dma((4,)), dma((6,)),
+            dma((RING,)), dma((ACT_SLOTS,)), dma((2,)), dma((2,)), dma((2,)), dma((4,)), dma((6,)), dma,
         ],
         compiler_params=pltpu.CompilerParams(vmem_limit_bytes=VMEM_MAX),
         name="ffn",
@@ -629,7 +638,7 @@
 
         m_new, v_new, w_new, gathered = exchange(
             tiles(g_emb, D), tiles(g_attn, D), tiles(g_in, FF), tiles(g_out, D),
-            g_vecd.reshape(-1, LANES), g_vecf.reshape(-1, LANES), opt_m.reshape(SHARD, LANES),
+            g_vecd.reshape(9, 1, D), g_vecf.reshape(-1, LANES), opt_m.reshape(SHARD, LANES),
             opt_v.reshape(SHARD, LANES), master.reshape(SHARD, LANES))
         flat = gathered.reshape(DEVICES, PAD, LANES)
         y_out, wb_emb, wb_attn, wb_in, wb_out, wb_vecd, wb_vecf, m_new, v_new, w_new = ffn(

time: 298 us -> 295 us (0.990)
  no operation moved by 1% of the time
where the time goes in v6:
time: 295 us; the launch traced here: 294 us
  Pallas kernels  294 us (100%)
    pallas_call x1, Pallas kernels, exchange(): pl.pallas_call(exchange_kernel, out_shape=(state_shape, state_shape, stat...  152 us
    pallas_call x1, Pallas kernels, ffn(): pl.pallas_call(functools.partial(ffn_kernel, steps), out_shape=(shape((to...  142 us

profile of v6, /device:TPU:0, one launch (start us, length us, event | category | flops | bytes accessed | tf_op | source)
XLA Modules:
  0.0 294.5 jit_solution(12234140349290734900)
XLA Ops:
  0.6 151.5 %exchange.1 = (f32[3461,128]{1,0:T(8,128)}, f32[3461,128]{1,0:T(8,128)}, f32[3461,128]{1,0:T(8,128)}, bf16[8,2,3472,128]{3,2,1,0:T(8,128)(2,1)}) custom-call(f32[1536,8,128]{2,1,0:T(8,128)} %bitcast.35, f32[2304,8,128]{2,1,0:T(8,128)} %bitcast.34, f32[1536,8,128]{2,1,0:T(8,128)} %bitcast.36, f32[1536,8,128]{2,1,0:T(8,128)} %bitcast.37, ...), custom_call_target="tpu_custom_call" | custom-call | tf_op jit(solution)/shard_map/exchange/pallas_call | solution.py:369
  152.2 142.1 %ffn.1 = (bf16[16384,768]{1,0:T(8,128)(2,1)}, bf16[2048,768]{1,0:T(8,128)(2,1)}, bf16[3072,768]{1,0:T(8,128)(2,1)}, bf16[768,2048]{1,0:T(8,128)(2,1)}, bf16[2048...) custom-call(s32[16384]{0:T(1024)} %ids_in.1, ...), custom_call_target="tpu_custom_call" | custom-call | tf_op jit(solution)/shard_map/ffn/pallas_call | solution.py:598

commit v7 on v6

--- a/solution.py
+++ b/solution.py
@@ -97,10 +97,13 @@
             index = index + WEIGHT[axis] * ((1 - mine[axis]) if axis in CHIP_ORDER[n] else mine[axis])
         return index
 
-    sequence = [(False, 0)]
-    for n in range(1, 8):
+    sequence = [(False, 0), (True, 0), (False, 1)]
+    for n in range(2, 8):
         sequence += [(False, n), (True, n - 1)]
     sequence.append((True, 7))
+
+    def slot_at(own, n):
+        return chip_at(7 if n == 0 and not own else n)
 
     def shard_at(place):
         own, n = sequence[place]
@@ -155,7 +158,7 @@
         owner = shard_at(place)
         low, high = chunk_bounds(owner)
         slot = place % STAGES
-        where = chip_at(sequence[place][1])
+        where = slot_at(*sequence[place])
 
         def one(k, carry):
             at = k - low
@@ -185,9 +188,8 @@
             acc[where, third:MARGIN + SHARD, :] = jnp.zeros((MARGIN + SHARD - third, LANES), jnp.float32)
 
     def pair_copy(n, part):
-        where = chip_at(n)
         return pltpu.make_async_remote_copy(
-            src_ref=acc.at[where, acc_rows(part)], dst_ref=pair.at[where, rows(part)],
+            src_ref=acc.at[slot_at(False, n), acc_rows(part)], dst_ref=pair.at[chip_at(n), rows(part)],
             send_sem=pair_send.at[n, part], recv_sem=pair_recv.at[n, part],
             device_id=peers["c"], device_id_type=MESH)
 
@@ -212,14 +214,13 @@
             send_sem=eighth_send.at[part], recv_sem=eighth_recv.at[part],
             device_id=peers[ORDERS[part][2]], device_id_type=MESH)
 
-    for place in range(STAGES):
-        load_shard(place)
-    for copy in vec_loads:
-        copy.start()
     barrier = pltpu.get_barrier_semaphore()
     for peer in peers.values():
         pl.semaphore_signal(barrier, inc=1, device_id=peer, device_id_type=MESH)
-    pl.semaphore_wait(barrier, 4)
+    for copy in vec_loads:
+        copy.start()
+    for place in range(STAGES):
+        load_shard(place)
     for copy in vec_loads:
         copy.wait()
     for i in range(9):
@@ -227,23 +228,32 @@
             row = i * (D // LANES) + j
             vecd_buf[row:row + 1, :] = vecd_raw[i, :, j * LANES:(j + 1) * LANES]
 
-    for place, (own, n) in enumerate(sequence):
-        if own:
-            for part in parts:
-                pair_copy(n, part).wait_send()
-        flatten_shard(place)
-        if place + STAGES < len(sequence):
-            load_shard(place + STAGES)
+    def join(n):
         where = chip_at(n)
         for part in parts:
-            if not own:
-                pair_copy(n, part).start()
-                continue
             pair_copy(n, part).wait_recv()
             acc[where, acc_rows(part)] += pair[where, rows(part)]
             bits = tuple(int(axis in CHIP_ORDER[n]) for axis in ORDERS[part])
             if bits[0]:
                 half_copy(HALF_ORDER.index(bits[1:]), part).start()
+
+    for place, (own, n) in enumerate(sequence):
+        sent = n if own else 0
+        if (own and n > 0) or (not own and n == 7):
+            for part in parts:
+                pair_copy(sent, part).wait_send()
+        flatten_shard(place)
+        if place == 0:
+            pl.semaphore_wait(barrier, 4)
+        if not own:
+            for part in parts:
+                pair_copy(n, part).start()
+        if place + STAGES < len(sequence):
+            load_shard(place + STAGES)
+        if own and n > 0:
+            join(n)
+        elif (own, n) == (False, 1):
+            join(0)
     for copy in state:
         copy.start()
     for k in range(4):

time: 295 us -> 291 us (0.986)
  Pallas kernels: 294 us -> 290 us
    pallas_call x1, Pallas kernels: 152 us -> 147 us  [exchange(): pl.pallas_call(exchange_kernel, out_shape=(state_shape, state_shape, stat...]
where the time goes in v7:
time: 291 us; the launch traced here: 290 us
  Pallas kernels  290 us (100%)
    pallas_call x1, Pallas kernels, exchange(): pl.pallas_call(exchange_kernel, out_shape=(state_shape, state_shape, stat...  147 us
    pallas_call x1, Pallas kernels, ffn(): pl.pallas_call(functools.partial(ffn_kernel, steps), out_shape=(shape((to...  142 us

profile of v7, /device:TPU:0, one launch (start us, length us, event | category | flops | bytes accessed | tf_op | source)
XLA Modules:
  0.0 290.4 jit_solution(14364232518617044590)
XLA Ops:
  0.6 147.5 %exchange.1 = (f32[3461,128]{1,0:T(8,128)}, f32[3461,128]{1,0:T(8,128)}, f32[3461,128]{1,0:T(8,128)}, bf16[8,2,3472,128]{3,2,1,0:T(8,128)(2,1)}) custom-call(f32[1536,8,128]{2,1,0:T(8,128)} %bitcast.35, f32[2304,8,128]{2,1,0:T(8,128)} %bitcast.34, f32[1536,8,128]{2,1,0:T(8,128)} %bitcast.36, f32[1536,8,128]{2,1,0:T(8,128)} %bitcast.37, ...), custom_call_target="tpu_custom_call" | custom-call | tf_op jit(solution)/shard_map/exchange/pallas_call | solution.py:379
  148.2 142.1 %ffn.1 = (bf16[16384,768]{1,0:T(8,128)(2,1)}, bf16[2048,768]{1,0:T(8,128)(2,1)}, bf16[3072,768]{1,0:T(8,128)(2,1)}, bf16[768,2048]{1,0:T(8,128)(2,1)}, bf16[2048...) custom-call(s32[16384]{0:T(1024)} %ids_in.1, ...), custom_call_target="tpu_custom_call" | custom-call | tf_op jit(solution)/shard_map/ffn/pallas_call | solution.py:608

commit v8 on v7

--- a/solution.py
+++ b/solution.py
@@ -412,12 +412,7 @@
 
     def store_y(it):
         return pltpu.make_async_copy(
-            y_buf.at[lax.rem(it, 2)], y_out.at[pl.ds(it * CHUNK - SUB, CHUNK)], y_sem.at[lax.rem(it, 2)])
-
-    store_first = pltpu.make_async_copy(
-        y_buf.at[0, pl.ds(SUB, CHUNK - SUB)], y_out.at[pl.ds(0, CHUNK - SUB)], y_sem.at[0])
-    store_last = pltpu.make_async_copy(
-        y_buf.at[steps % 2, pl.ds(0, SUB)], y_out.at[pl.ds(steps * CHUNK - SUB, SUB)], y_sem.at[steps % 2])
+            y_buf.at[lax.rem(it, 2)], y_out.at[pl.ds(it * CHUNK, CHUNK)], y_sem.at[lax.rem(it, 2)])
 
     def store_emb(it):
         return pltpu.make_async_copy(
@@ -454,7 +449,7 @@
             dense[pl.ds(at + row, 16), :] = ring[slot, pl.ds(row, 16), :].astype(jnp.float32)
             return carry
 
-        lax.fori_loop(0, whole, widen, 0, unroll=24)
+        lax.fori_loop(0, whole, widen, 0, unroll=31)
         tail = ring[n % RING, whole * 16:whole * 16 + 16, :].astype(jnp.float32)
         dense[at + whole * 16:at + SHARD, :] = tail[:SHARD - whole * 16]
         if n + RING < DEVICES:
@@ -538,16 +533,9 @@
         def _():
             load_act(it * UNROLL + 2 * UNROLL).start()
 
-        @pl.when(it == 2)
-        def _():
-            store_first.wait()
-
-        @pl.when(it > 2)
+        @pl.when(it >= 2)
         def _():
             store_y(it - 2).wait()
-
-        @pl.when(it >= 2)
-        def _():
             store_emb(it - 2).wait()
             store_attn(it - 2).wait()
 
@@ -561,33 +549,22 @@
         buffers = ((h_one, rows_one, u_one), (h_two, rows_two, u_two))
         for part in range(UNROLL):
             h_now, _, u_now = buffers[part % 2]
-            h_next, rows_next, u_before = buffers[(part + 1) % 2]
+            h_next, rows_next, _ = buffers[(part + 1) % 2]
             lookup(it * UNROLL + part + 1, h_next, rows_next)
             widen_tokens(h_now, u_now)
-            narrow_tokens(it, part, u_before)
+            narrow_tokens(it, part, u_now)
         for t in range(emb_rows // 16):
             relayout(TENSORS[0][2], D // LANES, it * emb_rows + t * 16, emb_buf.at[lax.rem(it, 2)], t * 16)
         for t in range(attn_rows // 16):
             relayout(TENSORS[1][2], D // LANES, it * attn_rows + t * 16, attn_buf.at[lax.rem(it, 2)], t * 16)
-        @pl.when(it == 0)
-        def _():
-            store_first.start()
-
-        @pl.when(it > 0)
-        def _():
-            store_y(it).start()
-
+        store_y(it).start()
         store_emb(it).start()
         store_attn(it).start()
         return carry
 
     lax.fori_loop(0, steps, body, 0)
-    store_y(steps - 2).wait()
-    narrow_tokens(steps, 0, u_two)
-    store_last.start()
-    store_y(steps - 1).wait()
-    store_last.wait()
     for it in (steps - 2, steps - 1):
+        store_y(it).wait()
         store_emb(it).wait()
         store_attn(it).wait()
     moves[-1].wait()

time: 291 us -> 291 us (level)
  no operation moved by 1% of the time
where the time goes in v8:
time: 291 us
  Pallas kernels  290 us (100%)
    pallas_call x1, Pallas kernels, exchange(): pl.pallas_call(exchange_kernel, out_shape=(state_shape, state_shape, stat...  147 us
    pallas_call x1, Pallas kernels, ffn(): pl.pallas_call(functools.partial(ffn_kernel, steps), out_shape=(shape((to...  143 us

profile of v8, /device:TPU:0, one launch (start us, length us, event | category | flops | bytes accessed | tf_op | source)
XLA Modules:
  0.0 290.9 jit_solution(8748164883380665372)
XLA Ops:
  0.6 147.5 %exchange.1 = (f32[3461,128]{1,0:T(8,128)}, f32[3461,128]{1,0:T(8,128)}, f32[3461,128]{1,0:T(8,128)}, bf16[8,2,3472,128]{3,2,1,0:T(8,128)(2,1)}) custom-call(f32[1536,8,128]{2,1,0:T(8,128)} %bitcast.35, f32[2304,8,128]{2,1,0:T(8,128)} %bitcast.34, f32[1536,8,128]{2,1,0:T(8,128)} %bitcast.36, f32[1536,8,128]{2,1,0:T(8,128)} %bitcast.37, ...), custom_call_target="tpu_custom_call" | custom-call | tf_op jit(solution)/shard_map/exchange/pallas_call | solution.py:379
  148.2 142.6 %ffn.1 = (bf16[16384,768]{1,0:T(8,128)(2,1)}, bf16[2048,768]{1,0:T(8,128)(2,1)}, bf16[3072,768]{1,0:T(8,128)(2,1)}, bf16[768,2048]{1,0:T(8,128)(2,1)}, bf16[2048...) custom-call(s32[16384]{0:T(1024)} %ids_in.1, ...), custom_call_target="tpu_custom_call" | custom-call | tf_op jit(solution)/shard_map/ffn/pallas_call | solution.py:585
